TPU v7x, 128 devices: a whole 4x4x4 slice. The times are simulated.
128 devices in a mesh: gx: 8 (over x, core), gy: 16 (over y, z).
Axes of the slice: x: 4, y: 4, z: 4, core: 2. Of those that a mesh axis runs over, the one named last changes fastest.
Arguments:
- slot_tiles: int32 [128, 128], P(('gx', 'gy')), may hold values from -1 to 255, as said below
- owner_map: int32 [128], replicated, may hold values from 0 to 127, each once
- slot_depth: int32 [128, 128, 16, 128], P(('gx', 'gy')), may hold values from 0 to 1073741823
- slot_color: bfloat16 [128, 128, 16, 3, 128], P(('gx', 'gy')), may hold values from 0 to 1
Outputs:
- region_depth: int32 [128, 2, 16, 128], P(('gx', 'gy'))
- region_color: bfloat16 [128, 2, 16, 3, 128], P(('gx', 'gy'))
- thumbnail: float32 [128, 3, 64], replicated
Inputs may be any that keep to these rules, and one draw needn't show every extreme that they name: `slot_tiles`: each rank's used slots name the tiles of one rectangle of at least 8 tile rows of the 16 x 16 tile grid, each once, in row-major order, followed by -1 in the unused slots; all ranks' rectangles contain a common region. `owner_map`: each rank owns exactly one region.
All inputs are finite; a program needn't handle non-finite values.
Results may differ from a plain program's by a relative error of at most 0.001.
Values may be sent and summed in bfloat16 or wider, within the bound.
A program may use at most 64 MiB of HBM per device.

v0:
```python
import jax
import jax.numpy as jnp
from jax import lax
from jax.sharding import Mesh
from jax.sharding import PartitionSpec as P

GX = ("gx_0", "gx_1")
GY = ("gy_0", "gy_1")
GX_GY = ("gx_0", "gx_1", "gy_0", "gy_1")


far_depth = 1073741824


def joined_along(tiles, dim):
    tiles = jnp.moveaxis(tiles, 0, dim)
    lengths = tiles.shape
    return tiles.reshape(*lengths[:dim], lengths[dim] * lengths[dim + 1], *lengths[dim + 2 :])


def all_blocks(shard, axes, turns):
    tiles = shard[None]
    for k in turns:
        tiles = lax.all_gather(tiles, axes[k], axis=0, tiled=True)
    held = [lax.axis_size(axes[k]) for k in reversed(turns)]
    tiles = tiles.reshape(*held, *shard.shape)
    turned = sorted(range(len(turns)), key=lambda place: turns[len(turns) - 1 - place])
    return tiles.transpose(*turned, *range(len(turns), tiles.ndim)).reshape(-1, *shard.shape)


def gather_axes(shard, axes, turns, dim):
    return joined_along(all_blocks(shard, axes, turns), dim)


def composite(pieces):
    depth_stack, color_stack = pieces
    nearest = jnp.min(depth_stack, axis=0)
    winner = jnp.argmin(depth_stack, axis=0)
    stack_index = lax.broadcasted_iota(jnp.int32, depth_stack.shape, 0)
    chosen = jnp.expand_dims(stack_index == winner[None], -2)
    masked = jnp.where(chosen, color_stack, jnp.zeros((), color_stack.dtype))
    picked = jnp.max(masked, axis=0)
    return (nearest, picked)


def pack_tiles(slot_tiles, owner_map, slot_depth, slot_color):
    grid_rows = lax.axis_size(GX)
    grid_cols = lax.axis_size(GY)
    region_count = grid_rows * grid_cols
    slot_count = slot_tiles.shape[1]
    tile_ids = slot_tiles[0]
    is_live = tile_ids >= 0
    safe_tile = jnp.where(is_live, tile_ids, 0)
    tile_row = safe_tile // grid_cols
    tile_col = safe_tile % grid_cols
    tile_region = tile_row // 2 * grid_cols + tile_col
    tile_half = tile_row % 2
    owner_rank = owner_map[tile_region]
    position = owner_rank * 2 + tile_half
    position = jnp.where(is_live, position, 2 * region_count)
    source_slot = jnp.full((2 * region_count + 1,), slot_count, jnp.int32)
    source_slot = source_slot.at[position].set(jnp.arange(slot_count, dtype=jnp.int32))[
        : 2 * region_count
    ]
    has_slot = source_slot < slot_count
    safe_slot = jnp.minimum(source_slot, slot_count - 1)
    rows_depth = jnp.take(slot_depth[0], safe_slot, axis=0)
    rows_color = jnp.take(slot_color[0], safe_slot, axis=0)
    send_depth = jnp.where(has_slot[:, None, None], rows_depth, far_depth)
    send_color = jnp.where(has_slot[:, None, None, None], rows_color, jnp.zeros((), jnp.bfloat16))
    return (send_depth, send_color)


def shards(slot_tiles, owner_map, slot_depth, slot_color):
    grid_rows = lax.axis_size(GX)
    grid_cols = lax.axis_size(GY)
    band_rows = slot_depth.shape[2]
    tile_width = slot_depth.shape[3]
    send_depth, send_color = pack_tiles(slot_tiles, owner_map, slot_depth, slot_color)
    send_depth = send_depth.reshape(grid_rows * grid_cols, 2, band_rows, tile_width)
    send_color = send_color.reshape(grid_rows * grid_cols, 2, band_rows, 3, tile_width)
    merged_depth, merged_color = composite(
        (
            lax.all_to_all(send_depth, GX_GY, split_axis=0, concat_axis=0, tiled=True),
            lax.all_to_all(send_color, GX_GY, split_axis=0, concat_axis=0, tiled=True),
        )
    )
    block_means = (
        merged_color.astype(jnp.float32)
        .reshape(2, band_rows // 8, 8, 3, tile_width // 8, 8)
        .mean(axis=(2, 5))
    )
    thumb_rows = jnp.transpose(block_means, (2, 0, 1, 3)).reshape(3, -1)
    gathered = gather_axes(thumb_rows[None], GX_GY, (0, 2, 3, 1), 0)
    thumbnail = gathered[owner_map]
    return (merged_depth[None], merged_color[None], thumbnail)


def solution(mesh):
    torus = Mesh(mesh.devices.reshape(4, 2, 4, 4), ("gx_0", "gx_1", "gy_0", "gy_1"))
    return jax.shard_map(
        shards,
        mesh=torus,
        in_specs=(
            P(GX_GY, None),
            P(),
            P(GX_GY, None, None, None),
            P(GX_GY, None, None, None, None),
        ),
        out_specs=(P(GX_GY, None, None, None), P(GX_GY, None, None, None, None), P()),
        check_vma=False,
    )
```

profile of v0, /device:TPU:1, one launch (start us, length us, event | category | flops | bytes accessed | tf_op | source)
XLA Modules:
  0.0 142.7 jit_solution(2710264809351740855)
XLA Ops:
  0.6 0.0 copy-start
  0.6 0.8 fusion.4
  1.5 1.6 %gather_fusion = s32[128]{0:T(128)S(1)} fusion(s32[128]{0:T(128)} %param.5, s32[1024]{0:T(1024)S(1)} %pad_clamp_fusion.2), kind=kCustom, calls=%fused_computation | custom fusion | bytes 1536 | tf_op jit(solution)/shard_map/gather | solution.py:58
  3.0 0.7 fusion.5
  3.7 1.0 scatter_custom_fusion
  4.7 0.2 lt.72
  4.9 0.1 min.14
  5.1 3.3 %gather_fusion.1 = s32[256,16,128]{2,1,0:T(8,128)} fusion(s32[128,16,128]{2,1,0:T(8,128)} %bitcast.42, s32[1024]{0:T(1024)S(1)} %pad_clamp_fusion.1), kind=kCustom, calls=%fused_computation.1 | custom fusion | bytes 4195328 | tf_op jit(solution)/shard_map/jit(_take)/gather | solution.py:67
  8.4 4.2 %select_select_fusion.1 = s32[128,2,16,128]{3,2,1,0:T(8,128)} fusion(s32[128,2,16,128]{3,2,1,0:T(8,128)} %bitcast.41, pred[128,2]{1,0:T(8,128)(4,1)S(1)} %compare_and_fusion, pred[128,2]{1,0:T(8,128)(4,1)S(1)} %lt.72), kind=kLoop, calls=%fused_computation.9 | loop fusion | flops 1048576 | bytes 4194816 | tf_op jit(solution)/shard_map/jit(_where)/select_n | solution.py:69
  12.6 11.9 %all-to-all-start = ((s32[128,2,16,128]{3,2,1,0:T(8,128)}), s32[128,2,16,128]{3,2,1,0:T(8,128)}, u32[]{:S(2)}, u32[]{:S(2)}) async-start(s32[128,2,16,128]{3,2,1,0:T(8,128)} %select_select_fusion.1), calls=%async_computation | async-start | bytes 4194304 | tf_op jit(solution)/shard_map/all_to_all | solution.py:84
  24.6 0.0 copy-done
  24.6 2.7 %gather_fusion.2 = bf16[256,16,3,128]{3,1,2,0:T(8,128)(2,1)} fusion(bf16[128,16,3,128]{3,1,2,0:T(8,128)(2,1)S(1)} %bitcast.39, s32[1024]{0:T(1024)S(1)} %pad_clamp_fusion.1), kind=kCustom, calls=%fused_computation.2 | custom fusion | bytes 6292480 | tf_op jit(solution)/shard_map/jit(_take)/gather | solution.py:68
  27.3 3.4 %select_select_fusion = bf16[128,2,16,3,128]{4,2,3,1,0:T(8,128)(2,1)} fusion(bf16[128,2,16,3,128]{4,2,3,1,0:T(8,128)(2,1)} %bitcast.40, pred[128,2]{1,0:T(8,128)(4,1)S(1)} %compare_and_fusion, pred[128,2]{1,0:T(8,128)(4,1)S(1)} %lt.72), kind=kLoop, calls=%fused_computation.6 | loop fusion | flops 3145728 | bytes 6291968 | tf_op jit(solution)/shard_map/jit(_where)/select_n | solution.py:70
  30.7 0.0 copy-start.1
  30.7 22.9 %all-to-all-done = s32[128,2,16,128]{3,2,1,0:T(8,128)} async-done(((s32[128,2,16,128]{3,2,1,0:T(8,128)}), s32[128,2,16,128]{3,2,1,0:T(8,128)}, u32[]{:S(2)}, u32[]{:S(2)}) %all-to-all-start) | async-done | bytes 2097184 | tf_op jit(solution)/shard_map/all_to_all | solution.py:84
  53.6 5.9 %all-to-all-start.1 = ((bf16[128,2,16,3,128]{4,2,3,1,0:T(8,128)(2,1)}), bf16[128,2,16,3,128]{4,2,3,1,0:T(8,128)(2,1)}, u32[]{:S(2)}, u32[]{:S(2)}) async-start(bf16[128,2,16,3,128]{4,2,3,1,0:T(8,128)(2,1)} %select_select_fusion), calls=%async_computation.1 | async-start | bytes 6291456 | tf_op jit(solution)/shard_map/all_to_all | solution.py:85
  59.6 0.0 copy-done.1
  59.6 2.4 %reduce_min.9 = s32[2,16,128]{2,1,0:T(8,128)} reduce(s32[128,2,16,128]{3,2,1,0:T(8,128)} %all-to-all-done, s32[]{:T(128)} %constant.97.clone.1), dimensions={0}, to_apply=%region_1.2 | reduce | flops 520192 | bytes 2113540 | tf_op jit(solution)/shard_map/reduce_min | solution.py:37
  62.0 2.7 %iota_reduce_fusion = (s32[2,16,128]{2,1,0:T(8,128)}, s32[2,16,128]{2,1,0:T(8,128)S(1)}) fusion(s32[128,2,16,128]{3,2,1,0:T(8,128)} %all-to-all-done), kind=kLoop, calls=%fused_computation.7 | loop fusion | flops 3641344 | bytes 2129920 | tf_op jit(solution)/shard_map/composite/reduce | solution.py:38
  64.7 0.3 iota_compare_fusion
  65.0 35.1 %all-to-all-done.1 = bf16[128,2,16,3,128]{4,2,3,1,0:T(8,128)(2,1)} async-done(((bf16[128,2,16,3,128]{4,2,3,1,0:T(8,128)(2,1)}), bf16[128,2,16,3,128]{4,2,3,1,0:T(8,128)(2,1)}, u32[]{:S(2)}, u32[]{:S(2)}) %all-to-all-start.1) | async-done | bytes 3145760 | tf_op jit(solution)/shard_map/all_to_all | solution.py:85
  100.1 3.0 %select_reduce_fusion = bf16[2,16,3,128]{3,1,2,0:T(8,128)(2,1)S(1)} fusion(bf16[128,2,16,3,128]{4,2,3,1,0:T(8,128)(2,1)} %all-to-all-done.1, pred[128,2,16,128]{3,2,1,0:T(8,128)(4,1)S(1)} %iota_compare_fusion), kind=kLoop, calls=%fused_computation.5 | loop fusion | flops 3133440 | bytes 3694592 | tf_op jit(solution)/shard_map/reduce_max | solution.py:42
  103.1 0.0 copy-start.2
  103.1 0.4 reshape.236
  103.5 0.1 reduce_sum.9
  103.7 0.1 broadcast_in_dim_broadcast_in_dim_reshape.4
  103.8 8.1 %all_gather.12 = f32[4,1,3,64]{3,1,2,0:T(1,128)S(1)} all-gather(f32[1,1,3,64]{3,1,2,0:T(1,128)S(1)} %broadcast_in_dim_broadcast_in_dim_reshape.4), channel_id=1, replica_groups=mesh['gx_0'=4,'gx_1'=2,'gy_0'=4,'gy_1'=4] {'gx_0'}, dimensions={0}, use_global_device_ids=true | all-gather | bytes 3840 | tf_op jit(solution)/shard_map/all_gather | solution.py:24
  111.9 9.1 %all_gather.13 = f32[16,1,3,64]{3,1,2,0:T(1,128)S(1)} all-gather(f32[4,1,3,64]{3,1,2,0:T(1,128)S(1)} %all_gather.12), channel_id=1, replica_groups=mesh['gx_0'=4,'gx_1'=2,'gy_0'=4,'gy_1'=4] {'gy_0'}, dimensions={0}, use_global_device_ids=true | all-gather | bytes 15360 | tf_op jit(solution)/shard_map/all_gather | solution.py:24
  120.9 9.0 %all_gather.14 = f32[64,1,3,64]{3,1,2,0:T(1,128)S(1)} all-gather(f32[16,1,3,64]{3,1,2,0:T(1,128)S(1)} %all_gather.13), channel_id=1, replica_groups=mesh['gx_0'=4,'gx_1'=2,'gy_0'=4,'gy_1'=4] {'gy_1'}, dimensions={0}, use_global_device_ids=true | all-gather | bytes 61440 | tf_op jit(solution)/shard_map/all_gather | solution.py:24
  130.0 10.9 %all_gather.15 = f32[128,1,3,64]{3,1,2,0:T(1,128)S(1)} all-gather(f32[64,1,3,64]{3,1,2,0:T(1,128)S(1)} %all_gather.14), channel_id=1, replica_groups=mesh['gx_0'=4,'gx_1'=2,'gy_0'=4,'gy_1'=4] {'gx_1'}, dimensions={0}, use_global_device_ids=true | all-gather | bytes 147456 | tf_op jit(solution)/shard_map/all_gather | solution.py:24
  140.9 0.1 copy.12
  141.0 0.1 copy.13
  141.2 0.8 gather_fusion.3
  141.9 0.8 copy.14
  142.7 0.0 copy-done.2
  (10 shorter events, 0.1 us)
Async XLA Ops:
  0.6 24.0 %copy-start = (bf16[1,128,16,3,128]{4,2,3,1,0:T(8,128)(2,1)S(1)}, bf16[1,128,16,3,128]{4,2,3,1,0:T(8,128)(2,1)}, u32[]{:S(2)}) copy-start(bf16[1,128,16,3,128]{4,2,3,1,0:T(8,128)(2,1)} %param.7) | copy-start | bytes 4718596
  12.6 41.0 %all-to-all-start = ((s32[128,2,16,128]{3,2,1,0:T(8,128)}), s32[128,2,16,128]{3,2,1,0:T(8,128)}, u32[]{:S(2)}, u32[]{:S(2)}) async-start(s32[128,2,16,128]{3,2,1,0:T(8,128)} %select_select_fusion.1), calls=%async_computation | async-start | bytes 4194304 | tf_op jit(solution)/shard_map/all_to_all | solution.py:84
  30.7 28.9 %copy-start.1 = (s32[128]{0:T(128)S(1)}, s32[128]{0:T(128)}, u32[]{:S(2)}) copy-start(s32[128]{0:T(128)} %param.5) | copy-start | bytes 1540
  53.6 46.5 %all-to-all-start.1 = ((bf16[128,2,16,3,128]{4,2,3,1,0:T(8,128)(2,1)}), bf16[128,2,16,3,128]{4,2,3,1,0:T(8,128)(2,1)}, u32[]{:S(2)}, u32[]{:S(2)}) async-start(bf16[128,2,16,3,128]{4,2,3,1,0:T(8,128)(2,1)} %select_select_fusion), calls=%async_computation.1 | async-start | bytes 6291456 | tf_op jit(solution)/shard_map/all_to_all | solution.py:85
  103.1 39.6 %copy-start.2 = (bf16[2,16,3,128]{3,1,2,0:T(8,128)(2,1)}, bf16[2,16,3,128]{3,1,2,0:T(8,128)(2,1)S(1)}, u32[]{:S(2)}) copy-start(bf16[2,16,3,128]{3,1,2,0:T(8,128)(2,1)S(1)} %select_reduce_fusion) | copy-start | bytes 73732
where the time goes:
time: 143 us
  waiting for transfers between devices  58 us (41%)
  blocking collectives  37.2 us (26%)
  starting transfers between devices  17.9 us (13%)
  other arithmetic  17.7 us (12%)
  local copies, waits for them, and re-layouts  11.1 us (8%)
    all_gather x4, blocking collectives, all_blocks(): tiles = lax.all_gather(tiles, axes[k], axis=0, tiled=True)  37.2 us
    all_to_all x1, waiting for transfers between devices, shards(): lax.all_to_all(send_color, GX_GY, split_axis=0, concat_axis=0, tiled=True)  35.1 us
    all_to_all x1, waiting for transfers between devices, shards(): lax.all_to_all(send_depth, GX_GY, split_axis=0, concat_axis=0, tiled=True)  22.9 us
    all_to_all x1, starting transfers between devices, shards(): lax.all_to_all(send_depth, GX_GY, split_axis=0, concat_axis=0, tiled=True)  11.9 us
    all_to_all x1, starting transfers between devices, shards(): lax.all_to_all(send_color, GX_GY, split_axis=0, concat_axis=0, tiled=True)  5.95 us
    select_n x1, other arithmetic, pack_tiles(): send_depth = jnp.where(has_slot[:, None, None], rows_depth, far_depth)  4.24 us
    select_n x1, other arithmetic, pack_tiles(): jnp.where(has_slot[:, None, None, None], rows_color, jnp.zeros((), jnp.bf...  3.42 us
    gather x1, local copies, waits for them, and re-layouts, pack_tiles(): rows_depth = jnp.take(slot_depth[0], safe_slot, axis=0)  3.33 us
  transfers between devices with their start and end apart: 2, of which 2 were waited for; matrix products, arithmetic and copies ran while one was open for 8% of the time, Pallas kernels for 0%

commit v1 on v0

v1 whole, which is shorter than its diff:
```python
import jax
import jax.numpy as jnp
import numpy as np
from jax import lax
from jax.experimental import pallas as pl
from jax.experimental.pallas import tpu as pltpu
from jax.sharding import PartitionSpec as P

MESH = pl.DeviceIdType.MESH
FAR = 1073741824
ORDER = ((0, 1, 2), (1, 2, 0), (2, 0, 1))
STRIDE = (32, 4, 1)
COUNT = (3, 3, 2)
BASE = (0, 48, 96)
CLASS = ((0, 0, 3), (1, 1, 3), (2, 2))
HALF = ((0, 1, 0), (0, 1, 1), (0, 1))
CHUNKS = tuple((stream, off) for off in (1, 3, 2, 0) for stream in range(3))


def tile_places():
    places = np.zeros((1, 128), np.int32)
    for stream in range(3):
        first, second, third = ORDER[stream]
        count = COUNT[stream]
        for i in range(4):
            for j in range(4):
                for t in range(count):
                    at = [0, 0, 0]
                    at[first], at[second] = i, j
                    at[third] = (CLASS[stream][t] - i - j) % 4
                    owner = sum(a * s for a, s in zip(at, STRIDE))
                    places[0, BASE[stream] + (i * 4 + j) * count + t] = 2 * owner + HALF[stream][t]
    return places


def pick(mask, new, old):
    return jnp.where(mask[None], new, old)


def kernel(
    tiles_ref, owner_ref, place_ref, depth_hbm, color_hbm,
    depth_out, color_out, thumbs_out,
    in_d, in_c, table_v, table, send_d, send_c, got_d, got_c,
    own_d, own_c, one_d, one_c, out1_d, out1_c, two_d, two_c, out2_d, out2_c,
    last_d, last_c, thumbs,
    load_sem, table_sem, core_send, core_recv, send1, recv1, send2, recv2, send3, recv3,
    thumb_send, thumb_recv, store_sem,
):
    gx, gy = lax.axis_index("gx"), lax.axis_index("gy")
    core = lax.rem(gx, 2)
    at = (lax.div(gx, 2), lax.div(gy, 4), lax.rem(gy, 4))
    me = gx * 16 + gy

    def device(x, y, z, c=core):
        return (2 * x + c, 4 * y + z)

    def peer(axis, off):
        moved = [lax.rem(a + off, 4) if k == axis else a for k, a in enumerate(at)]
        return device(*moved)

    partner = device(*at, c=1 - core)

    loads = [
        pltpu.make_async_copy(depth_hbm, in_d.at[pl.ds(0, 128)], load_sem.at[0]),
        pltpu.make_async_copy(color_hbm, in_c.at[pl.ds(0, 128)], load_sem.at[1]),
    ]
    for load in loads:
        load.start()
    barrier = pltpu.get_barrier_semaphore()
    pl.semaphore_signal(barrier, inc=1, device_id=partner, device_id_type=MESH)
    for axis in range(3):
        for off in (1, 2, 3):
            pl.semaphore_signal(barrier, inc=1, device_id=peer(axis, off), device_id_type=MESH)

    in_d[128] = jnp.full((16, 128), FAR, jnp.int32)
    in_c[128] = jnp.zeros((3, 16, 128), jnp.bfloat16)
    tiles = tiles_ref[...]
    live = tiles >= 0
    row = lax.shift_right_arithmetic(tiles, 4)
    region = lax.shift_right_arithmetic(row, 1) * 16 + (tiles & 15)
    down = lax.broadcasted_iota(jnp.int32, (128, 128), 0)
    owner_down = jnp.transpose(jnp.broadcast_to(owner_ref[...], (128, 128)))
    owner = jnp.sum(jnp.where(down == region, owner_down, 0), axis=0, keepdims=True)
    place = jnp.where(live, 2 * owner + (row & 1), -1)
    place_down = jnp.transpose(jnp.broadcast_to(place, (128, 128)))
    for c in range(2):
        hit = place_down == place_ref[...] + 32 * c
        table_v[c : c + 1, :] = jnp.min(jnp.where(hit, down, 128), axis=0, keepdims=True)
    to_table = pltpu.make_async_copy(table_v, table, table_sem)
    to_table.start()
    to_table.wait()
    for load in loads:
        load.wait()
    pl.semaphore_wait(barrier, 10)

    def remote(src, dst, sends, recvs, index, target):
        copy = pltpu.make_async_remote_copy(
            src_ref=src, dst_ref=dst, send_sem=sends.at[index], recv_sem=recvs.at[index],
            device_id=target, device_id_type=MESH,
        )
        copy.start()
        return copy

    def chunk(stream, off):
        size = 4 * COUNT[stream]
        return BASE[stream] + lax.rem(at[ORDER[stream][0]] + off, 4) * size, size

    core_copies = []
    for n, (stream, off) in enumerate(CHUNKS):
        start, size = chunk(stream, off)

        def pack(t, carry):
            q = start + t
            slot = table[1 - core, q]
            send_d[q] = in_d[slot]
            send_c[q] = in_c[slot]
            return carry

        lax.fori_loop(0, size, pack, 0, unroll=4)
        part = pl.ds(start, size)
        core_copies.append((
            remote(send_d.at[part], got_d.at[part], core_send, core_recv, 2 * n, partner),
            remote(send_c.at[part], got_c.at[part], core_send, core_recv, 2 * n + 1, partner),
        ))

    copies1 = {}
    for n, (stream, off) in enumerate(CHUNKS):
        start, size = chunk(stream, off)
        for copy in core_copies[n]:
            copy.wait_recv()
        to_d, to_c = (own_d, own_c) if off else (one_d, one_c)

        def meet(t, carry):
            q = start + t
            slot = table[core, q]
            mine = (in_d[slot] - FAR) * 2 + core
            other = (got_d[q] - FAR) * 2 + (1 - core)
            nearer = other < mine
            to_d[q] = jnp.where(nearer, other, mine)
            to_c[q] = pick(nearer, got_c[q], in_c[slot])
            return carry

        lax.fori_loop(0, size, meet, 0, unroll=2)
        if off:
            axis = ORDER[stream][0]
            src = pl.ds(start, size)
            dst = pl.ds(BASE[stream] + at[axis] * size, size)
            index = 2 * (3 * stream + off - 1)
            copies1[stream, off] = (
                remote(own_d.at[src], one_d.at[dst], send1, recv1, index, peer(axis, off)),
                remote(own_c.at[src], one_c.at[dst], send1, recv1, index + 1, peer(axis, off)),
            )

    copies2 = {}
    for stream in range(3):
        first, second, third = ORDER[stream]
        count, base = COUNT[stream], BASE[stream]
        for off in (1, 2, 3):
            for copy in copies1[stream, off]:
                copy.wait_recv()
        rest = at[second] * STRIDE[second] + at[third] * STRIDE[third]
        for off in (1, 2, 3, 0):
            to = lax.rem(at[second] + off, 4)
            if off:
                to_d, to_c, into = out1_d, out1_c, base // 4 + (off - 1) * count
            else:
                to_d, to_c, into = two_d, two_c, base // 4 + at[second] * count

            def join(t, carry):
                key = tag = color = best = None
                for src in range(4):
                    q = base + src * 4 * count + to * count + t
                    k = one_d[q]
                    depth = lax.shift_right_arithmetic(k, 1)
                    order = depth if first == 0 else k
                    rank = rest + src * STRIDE[first] + (k & 1) * 16
                    if src == 0:
                        key, best, tag, color = order, depth, rank, one_c[q]
                    else:
                        nearer = order < key
                        key = jnp.where(nearer, order, key)
                        best = jnp.where(nearer, depth, best)
                        tag = jnp.where(nearer, rank, tag)
                        color = pick(nearer, one_c[q], color)
                to_d[into + t] = best
                to_c[into + t, 0:3] = color
                to_c[into + t, 3] = tag.astype(jnp.float32).astype(jnp.bfloat16)
                return carry

            lax.fori_loop(0, count, join, 0)
            if off:
                src = pl.ds(into, count)
                dst = pl.ds(base // 4 + at[second] * count, count)
                index = 2 * (3 * stream + off - 1)
                copies2[stream, off] = (
                    remote(out1_d.at[src], two_d.at[dst], send2, recv2, index, peer(second, off)),
                    remote(out1_c.at[src], two_c.at[dst], send2, recv2, index + 1, peer(second, off)),
                )

    def closer(depth, color, best, kept):
        tag, old = color[3].astype(jnp.float32), kept[3].astype(jnp.float32)
        nearer = (depth < best) | ((depth == best) & (tag < old))
        return jnp.where(nearer, depth, best), pick(nearer, color, kept)

    for stream in range(3):
        count, base = COUNT[stream], BASE[stream] // 4
        for off in (1, 2, 3):
            for copy in copies2[stream, off]:
                copy.wait_recv()
        for t in range(count):
            best, kept = two_d[base + t], two_c[base + t]
            for src in (1, 2, 3):
                q = base + src * count + t
                best, kept = closer(two_d[q], two_c[q], best, kept)
            k = 2 * CLASS[stream][t] + HALF[stream][t]
            out2_d[k] = best
            out2_c[k] = kept

    x, y, z = at
    mine = lax.rem(x + y + z, 4)
    copies3 = {}
    for off in (1, 2, 3):
        theirs = lax.rem(mine + off, 4)
        for half in range(2):
            along_z = (theirs == 0) | ((theirs == 3) & (half == 0))
            along_y = theirs == 2
            along_x = (theirs == 1) | ((theirs == 3) & (half == 1))
            target = device(
                lax.rem(x + jnp.where(along_x, off, 0), 4),
                lax.rem(y + jnp.where(along_y, off, 0), 4),
                lax.rem(z + jnp.where(along_z, off, 0), 4),
            )
            k = 2 * theirs + half
            slot = 3 * half + off - 1
            copies3[half, off] = (
                remote(out2_d.at[k], last_d.at[slot], send3, recv3, 2 * slot, target),
                remote(out2_c.at[k], last_c.at[slot], send3, recv3, 2 * slot + 1, target),
            )

    sums = []
    for half in range(2):
        best, kept = out2_d[2 * mine + half], out2_c[2 * mine + half]
        for off in (1, 2, 3):
            for copy in copies3[half, off]:
                copy.wait_recv()
            slot = 3 * half + off - 1
            best, kept = closer(last_d[slot], last_c[slot], best, kept)
        depth_out[half] = best + FAR
        color_out[half] = kept[0:3]
        sums.append(jnp.sum(kept[0:3].astype(jnp.float32).reshape(3, 2, 8, 128), axis=2))
    rows = jnp.concatenate(
        [s for c in range(3) for s in (sums[0][c], sums[1][c])] + [jnp.zeros((4, 128), jnp.float32)], axis=0
    )
    lane_down = lax.broadcasted_iota(jnp.int32, (128, 128), 0)
    lane = lax.broadcasted_iota(jnp.int32, (128, 128), 1)
    spread = jnp.where(lax.shift_right_logical(lane_down, 3) == (lane & 15), 1.0 / 64, 0.0)
    means = jnp.dot(rows, spread, precision=lax.Precision.HIGHEST, preferred_element_type=jnp.float32)
    line = lax.broadcasted_iota(jnp.int32, (16, 128), 0) & 7
    group = lax.shift_right_logical(lax.broadcasted_iota(jnp.int32, (16, 128), 1), 4)
    thumbs[me] = jnp.sum(jnp.where(line == group, means, 0.0).reshape(2, 8, 128), axis=1)

    def tell(i, carry):
        other = lax.rem(me + i, 128)
        pltpu.make_async_remote_copy(
            src_ref=thumbs.at[me], dst_ref=thumbs.at[me], send_sem=thumb_send, recv_sem=thumb_recv,
            device_id=(lax.div(other, 16), lax.rem(other, 16)), device_id_type=MESH,
        ).start()
        return carry

    lax.fori_loop(1, 128, tell, 0)
    for group_of in (core_copies, copies1.values(), copies2.values(), copies3.values()):
        for pair in group_of:
            for copy in pair:
                copy.wait_send()
    most = thumbs.at[pl.ds(0, 127)]
    pltpu.make_async_copy(most, most, thumb_recv).wait()
    pltpu.make_async_copy(most, most, thumb_send).wait()
    thumbs_out[...] = thumbs[...]


def shards(slot_tiles, owner_map, slot_depth, slot_color):
    i32, bf16 = jnp.int32, jnp.bfloat16
    vmem = pl.BlockSpec(memory_space=pltpu.VMEM)
    anywhere = pl.BlockSpec(memory_space=pl.ANY)
    dma = pltpu.SemaphoreType.DMA
    scratch = [
        pltpu.VMEM((129, 16, 128), i32), pltpu.VMEM((129, 3, 16, 128), bf16),
        pltpu.VMEM((2, 128), i32), pltpu.SMEM((2, 128), i32),
    ]
    for tiles, channels in ((128, 3), (128, 3), (128, 3), (128, 3), (32, 4), (32, 4), (8, 4), (6, 4)):
        scratch += [pltpu.VMEM((tiles, 16, 128), i32), pltpu.VMEM((tiles, channels, 16, 128), bf16)]
    scratch += [pltpu.VMEM((128, 2, 128), jnp.float32), dma((2,)), dma]
    scratch += [dma((24,)), dma((24,)), dma((18,)), dma((18,)), dma((18,)), dma((18,)), dma((12,)), dma((12,))]
    scratch += [dma, dma, dma]
    depth, color, thumbs = pl.pallas_call(
        kernel,
        out_shape=(
            jax.ShapeDtypeStruct((2, 16, 128), i32),
            jax.ShapeDtypeStruct((2, 3, 16, 128), bf16),
            jax.ShapeDtypeStruct((128, 2, 128), jnp.float32),
        ),
        in_specs=[vmem, vmem, vmem, anywhere, anywhere],
        out_specs=(vmem, vmem, vmem),
        scratch_shapes=scratch,
        compiler_params=pltpu.CompilerParams(collective_id=0, has_side_effects=True),
        name="composite",
    )(
        slot_tiles,
        owner_map[None],
        jnp.asarray(tile_places()),
        slot_depth[0],
        jnp.swapaxes(slot_color[0], 1, 2),
    )
    thumbnail = thumbs.reshape(128, 256)[:, :192][owner_map].reshape(128, 3, 64)
    return depth[None], jnp.swapaxes(color, 1, 2)[None], thumbnail


def solution(mesh):
    ranks = ("gx", "gy")
    return jax.shard_map(
        shards,
        mesh=mesh,
        in_specs=(P(ranks, None), P(), P(ranks, None, None, None), P(ranks, None, None, None, None)),
        out_specs=(P(ranks, None, None, None), P(ranks, None, None, None, None), P()),
        check_vma=False,
    )
```

time: 143 us -> 47.7 us (0.33)
  waiting for transfers between devices: 58 us -> 0 us
  Pallas kernels: 0 us -> 42.6 us
  blocking collectives: 37.2 us -> 0 us
  starting transfers between devices: 17.9 us -> 0 us
  other arithmetic: 17.7 us -> 0.67 us
  local copies, waits for them, and re-layouts: 11.1 us -> 3.64 us
    all_to_all x2 -> x0, waiting for transfers between devices: 58 us -> none  [the longest x1 35.1 us: shards(): lax.all_to_all(send_color, GX_GY, split_axis=0, concat_axis=0, tiled=True)]
    pallas_call x0 -> x1, Pallas kernels: none -> 42.6 us  [shards(): pl.pallas_call(kernel, out_shape=(jax.ShapeDtypeStruct((2, 16, 128), i32)...]
    all_gather x4 -> x0, blocking collectives: 37.2 us -> none  [all_blocks(): tiles = lax.all_gather(tiles, axes[k], axis=0, tiled=True)]
    all_to_all x2 -> x0, starting transfers between devices: 17.9 us -> none  [the longest x1 11.9 us: shards(): lax.all_to_all(send_depth, GX_GY, split_axis=0, concat_axis=0, tiled=True)]
    select_n x5 -> x1, other arithmetic: 9.13 us -> 0.66 us  [shards(): thumbnail = thumbs.reshape(128, 256)[:, :192][owner_map].reshape(128, 3, 64)]
    gather x4 -> x2, local copies, waits for them, and re-layouts: 8.34 us -> 1.5 us  [shards(): thumbnail = thumbs.reshape(128, 256)[:, :192][owner_map].reshape(128, 3, 64)]
    reduce_max x1 -> x0, other arithmetic: 2.96 us -> none  [composite(): picked = jnp.max(masked, axis=0)]
    another operation x1 -> x0, other arithmetic: 2.73 us -> none  [composite(): winner = jnp.argmin(depth_stack, axis=0)]
  transfers between devices with their start and end apart: 2 -> 0, of which waited for: 2 -> 0; matrix products, arithmetic and copies ran while one was open for 8% -> 0% of each run, Pallas kernels for 0% -> 0%
where the time goes in v1:
time: 47.7 us; the launch traced here: 47.6 us
  Pallas kernels  42.6 us (89%)
  local copies, waits for them, and re-layouts  3.64 us (8%)
  other arithmetic  0.67 us (1%)
  between operations  0.66 us (1%)
    pallas_call x1, Pallas kernels, shards(): pl.pallas_call(kernel, out_shape=(jax.ShapeDtypeStruct((2, 16, 128), i32)...  42.6 us
    unnamed x7, local copies, waits for them, and re-layouts  2.15 us
    gather x2, local copies, waits for them, and re-layouts, shards(): thumbnail = thumbs.reshape(128, 256)[:, :192][owner_map].reshape(128, 3, 64)  1.5 us

profile of v1, /device:TPU:1, one launch (start us, length us, event | category | flops | bytes accessed | tf_op | source)
XLA Modules:
  0.0 47.6 jit_solution(9503789762446320594)
XLA Ops:
  0.6 0.7 %compare_select_fusion = s32[128]{0:T(128)S(1)} fusion(s32[128]{0:T(128)} %param.6), kind=kLoop, calls=%fused_computation.3 | loop fusion | flops 384 | bytes 1024 | tf_op jit(solution)/shard_map/select_n | solution.py:314
  1.3 42.6 %composite.1 = (s32[2,16,128]{2,1,0:T(8,128)}, bf16[2,3,16,128]{3,2,1,0:T(8,128)(2,1)}, f32[128,2,128]{2,1,0:T(2,128)}) custom-call(s32[1,128]{1,0:T(1,128)} %tiles_ref.1, s32[1,128]{1,0:T(1,128)} %bitcast.22, s32[1,128]{1,0:T(1,128)} %constant.6.clone.place_ref, s32[128,16,128]{2,1,0:T(8,128)} %bitcast.17, bf16[128,3,16,128]{3,2,1,0:T(8,128)(2,1)} %bitcast.16), custom_call_target="tpu_custom_call" | custom-call | tf_op jit(solution)/shard_map/composite/pallas_call | solution.py:295
  43.9 0.0 copy-start.1
  43.9 0.0 copy-start
  43.9 0.9 %copy.12 = f32[16,8,2,128]{3,1,2,0:T(8,128)S(1)} copy(f32[16,8,2,128]{3,2,1,0:T(2,128)} %bitcast.18) | data formatting | bytes 262144
  44.8 0.8 %gather_fusion = f32[128,192]{1,0:T(8,128)S(1)} fusion(f32[128,192]{1,0:T(8,128)S(1)} %bitcast.15, s32[1024]{0:T(1024)S(1)} %pad_clamp_fusion), kind=kCustom, calls=%fused_computation | custom fusion | bytes 197120 | tf_op jit(solution)/shard_map/gather | solution.py:314
  45.6 0.7 %copy.9 = f32[128,192]{0,1:T(8,128)} copy(f32[128,192]{1,0:T(8,128)S(1)} %gather_fusion) | data formatting | bytes 196608 | tf_op jit(solution)/shard_map/gather | solution.py:314
  46.3 0.0 copy-done.1
  46.3 0.6 %copy.15 = s32[1,2,16,128]{3,2,1,0:T(8,128)} copy(s32[1,2,16,128]{3,2,1,0:T(8,128)S(1)} %bitcast.21) | data formatting | bytes 32768
  46.9 0.0 copy-done
  46.9 0.6 %copy.16 = bf16[1,2,16,3,128]{4,2,3,1,0:T(8,128)(2,1)} copy(bf16[1,2,16,3,128]{4,2,3,1,0:T(8,128)(2,1)S(1)} %bitcast.20) | data formatting | bytes 49152
  (1 shorter events, 0.0 us)
Async XLA Ops:
  43.9 2.5 %copy-start.1 = (s32[2,16,128]{2,1,0:T(8,128)S(1)}, s32[2,16,128]{2,1,0:T(8,128)}, u32[]{:S(2)}) copy-start(s32[2,16,128]{2,1,0:T(8,128)} %get-tuple-element.6) | copy-start | bytes 49156
  43.9 3.0 %copy-start = (bf16[2,3,16,128]{3,2,1,0:T(8,128)(2,1)S(1)}, bf16[2,3,16,128]{3,2,1,0:T(8,128)(2,1)}, u32[]{:S(2)}) copy-start(bf16[2,3,16,128]{3,2,1,0:T(8,128)(2,1)} %get-tuple-element.7) | copy-start | bytes 73732

commit v2 on v1

--- a/solution.py
+++ b/solution.py
@@ -15,6 +15,7 @@
 CLASS = ((0, 0, 3), (1, 1, 3), (2, 2))
 HALF = ((0, 1, 0), (0, 1, 1), (0, 1))
 CHUNKS = tuple((stream, off) for off in (1, 3, 2, 0) for stream in range(3))
+FAR_FIRST = sorted(np.ndindex(4, 4, 4), key=lambda d: -sum(min(a, 4 - a) for a in d))
 
 
 def tile_places():
@@ -29,7 +30,7 @@
                     at[first], at[second] = i, j
                     at[third] = (CLASS[stream][t] - i - j) % 4
                     owner = sum(a * s for a, s in zip(at, STRIDE))
-                    places[0, BASE[stream] + (i * 4 + j) * count + t] = 2 * owner + HALF[stream][t]
+                    places[0, BASE[stream] + (j * 4 + i) * count + t] = 2 * owner + HALF[stream][t]
     return places
 
 
@@ -103,7 +104,7 @@
 
     def chunk(stream, off):
         size = 4 * COUNT[stream]
-        return BASE[stream] + lax.rem(at[ORDER[stream][0]] + off, 4) * size, size
+        return BASE[stream] + lax.rem(at[ORDER[stream][1]] + off, 4) * size, size
 
     core_copies = []
     for n, (stream, off) in enumerate(CHUNKS):
@@ -126,76 +127,77 @@
     copies1 = {}
     for n, (stream, off) in enumerate(CHUNKS):
         start, size = chunk(stream, off)
+        axis, count = ORDER[stream][0], COUNT[stream]
         for copy in core_copies[n]:
             copy.wait_recv()
-        to_d, to_c = (own_d, own_c) if off else (one_d, one_c)
-
-        def meet(t, carry):
-            q = start + t
-            slot = table[core, q]
-            mine = (in_d[slot] - FAR) * 2 + core
-            other = (got_d[q] - FAR) * 2 + (1 - core)
-            nearer = other < mine
-            to_d[q] = jnp.where(nearer, other, mine)
-            to_c[q] = pick(nearer, got_c[q], in_c[slot])
-            return carry
-
-        lax.fori_loop(0, size, meet, 0, unroll=2)
-        if off:
-            axis = ORDER[stream][0]
-            src = pl.ds(start, size)
-            dst = pl.ds(BASE[stream] + at[axis] * size, size)
-            index = 2 * (3 * stream + off - 1)
-            copies1[stream, off] = (
-                remote(own_d.at[src], one_d.at[dst], send1, recv1, index, peer(axis, off)),
-                remote(own_c.at[src], one_c.at[dst], send1, recv1, index + 1, peer(axis, off)),
-            )
+        for step in (1, 3, 2, 0):
+            first = start + lax.rem(at[axis] + step, 4) * count
+            to_d, to_c = (own_d, own_c) if step else (one_d, one_c)
+
+            def meet(t, carry):
+                q = first + t
+                slot = table[core, q]
+                mine = (in_d[slot] - FAR) * 2 + core
+                other = (got_d[q] - FAR) * 2 + (1 - core)
+                nearer = other < mine
+                to_d[q] = jnp.where(nearer, other, mine)
+                to_c[q] = pick(nearer, got_c[q], in_c[slot])
+                return carry
+
+            lax.fori_loop(0, count, meet, 0, unroll=True)
+            if step:
+                src = pl.ds(first, count)
+                dst = pl.ds(start + at[axis] * count, count)
+                index = 2 * (3 * n + step - 1)
+                copies1[n, step] = (
+                    remote(own_d.at[src], one_d.at[dst], send1, recv1, index, peer(axis, step)),
+                    remote(own_c.at[src], one_c.at[dst], send1, recv1, index + 1, peer(axis, step)),
+                )
 
     copies2 = {}
-    for stream in range(3):
+    for n, (stream, off) in enumerate(CHUNKS):
+        start, size = chunk(stream, off)
         first, second, third = ORDER[stream]
-        count, base = COUNT[stream], BASE[stream]
-        for off in (1, 2, 3):
-            for copy in copies1[stream, off]:
+        count, base = COUNT[stream], BASE[stream] // 4
+        for step in (1, 3, 2):
+            for copy in copies1[n, step]:
                 copy.wait_recv()
         rest = at[second] * STRIDE[second] + at[third] * STRIDE[third]
-        for off in (1, 2, 3, 0):
-            to = lax.rem(at[second] + off, 4)
-            if off:
-                to_d, to_c, into = out1_d, out1_c, base // 4 + (off - 1) * count
-            else:
-                to_d, to_c, into = two_d, two_c, base // 4 + at[second] * count
-
-            def join(t, carry):
-                key = tag = color = best = None
-                for src in range(4):
-                    q = base + src * 4 * count + to * count + t
-                    k = one_d[q]
-                    depth = lax.shift_right_arithmetic(k, 1)
-                    order = depth if first == 0 else k
-                    rank = rest + src * STRIDE[first] + (k & 1) * 16
-                    if src == 0:
-                        key, best, tag, color = order, depth, rank, one_c[q]
-                    else:
-                        nearer = order < key
-                        key = jnp.where(nearer, order, key)
-                        best = jnp.where(nearer, depth, best)
-                        tag = jnp.where(nearer, rank, tag)
-                        color = pick(nearer, one_c[q], color)
-                to_d[into + t] = best
-                to_c[into + t, 0:3] = color
-                to_c[into + t, 3] = tag.astype(jnp.float32).astype(jnp.bfloat16)
-                return carry
-
-            lax.fori_loop(0, count, join, 0)
-            if off:
-                src = pl.ds(into, count)
-                dst = pl.ds(base // 4 + at[second] * count, count)
-                index = 2 * (3 * stream + off - 1)
-                copies2[stream, off] = (
-                    remote(out1_d.at[src], two_d.at[dst], send2, recv2, index, peer(second, off)),
-                    remote(out1_c.at[src], two_c.at[dst], send2, recv2, index + 1, peer(second, off)),
-                )
+        if off:
+            to_d, to_c, into = out1_d, out1_c, base + (off - 1) * count
+        else:
+            to_d, to_c, into = two_d, two_c, base + at[second] * count
+
+        def join(t, carry):
+            key = tag = color = best = None
+            for src in range(4):
+                q = start + src * count + t
+                k = one_d[q]
+                depth = lax.shift_right_arithmetic(k, 1)
+                order = depth if first == 0 else k
+                rank = rest + src * STRIDE[first] + (k & 1) * 16
+                if src == 0:
+                    key, best, tag, color = order, depth, rank, one_c[q]
+                else:
+                    nearer = order < key
+                    key = jnp.where(nearer, order, key)
+                    best = jnp.where(nearer, depth, best)
+                    tag = jnp.where(nearer, rank, tag)
+                    color = pick(nearer, one_c[q], color)
+            to_d[into + t] = best
+            to_c[into + t, 0:3] = color
+            to_c[into + t, 3] = tag.astype(jnp.float32).astype(jnp.bfloat16)
+            return carry
+
+        lax.fori_loop(0, count, join, 0)
+        if off:
+            src = pl.ds(into, count)
+            dst = pl.ds(base + at[second] * count, count)
+            index = 2 * (3 * stream + off - 1)
+            copies2[stream, off] = (
+                remote(out1_d.at[src], two_d.at[dst], send2, recv2, index, peer(second, off)),
+                remote(out1_c.at[src], two_c.at[dst], send2, recv2, index + 1, peer(second, off)),
+            )
 
     def closer(depth, color, best, kept):
         tag, old = color[3].astype(jnp.float32), kept[3].astype(jnp.float32)
@@ -259,15 +261,16 @@
     group = lax.shift_right_logical(lax.broadcasted_iota(jnp.int32, (16, 128), 1), 4)
     thumbs[me] = jnp.sum(jnp.where(line == group, means, 0.0).reshape(2, 8, 128), axis=1)
 
-    def tell(i, carry):
-        other = lax.rem(me + i, 128)
-        pltpu.make_async_remote_copy(
-            src_ref=thumbs.at[me], dst_ref=thumbs.at[me], send_sem=thumb_send, recv_sem=thumb_recv,
-            device_id=(lax.div(other, 16), lax.rem(other, 16)), device_id_type=MESH,
-        ).start()
-        return carry
-
-    lax.fori_loop(1, 128, tell, 0)
+    around = [[lax.rem(a + off, 4) for off in range(4)] for a in at]
+    across = [[2 * a + c for a in around[0]] for c in (core, 1 - core)]
+    along = [[4 * b + c for c in around[2]] for b in around[1]]
+    for dx, dy, dz in FAR_FIRST:
+        for other in range(2):
+            if dx or dy or dz or other:
+                pltpu.make_async_remote_copy(
+                    src_ref=thumbs.at[me], dst_ref=thumbs.at[me], send_sem=thumb_send, recv_sem=thumb_recv,
+                    device_id=(across[other][dx], along[dy][dz]), device_id_type=MESH,
+                ).start()
     for group_of in (core_copies, copies1.values(), copies2.values(), copies3.values()):
         for pair in group_of:
             for copy in pair:
@@ -276,6 +279,18 @@
     pltpu.make_async_copy(most, most, thumb_recv).wait()
     pltpu.make_async_copy(most, most, thumb_send).wait()
     thumbs_out[...] = thumbs[...]
+
+
+def settle(owner_ref, depth_ref, color_ref, thumbs_ref, depth_out, color_out, thumbs_out):
+    depth_out[...] = depth_ref[...]
+    color_out[...] = color_ref[...]
+    held = lax.broadcasted_iota(jnp.int32, (128, 128), 0) == owner_ref[...]
+    chosen = jnp.where(held, 1.0, 0.0)
+    for row, size in ((0, 128), (1, 64)):
+        thumbs_out[128 * row : 128 * row + size] = lax.dot_general(
+            thumbs_ref[:, row, 0:size], chosen, (((0,), (0,)), ((), ())),
+            precision=lax.Precision.HIGHEST, preferred_element_type=jnp.float32,
+        )
 
 
 def shards(slot_tiles, owner_map, slot_depth, slot_color):
@@ -290,14 +305,14 @@
     for tiles, channels in ((128, 3), (128, 3), (128, 3), (128, 3), (32, 4), (32, 4), (8, 4), (6, 4)):
         scratch += [pltpu.VMEM((tiles, 16, 128), i32), pltpu.VMEM((tiles, channels, 16, 128), bf16)]
     scratch += [pltpu.VMEM((128, 2, 128), jnp.float32), dma((2,)), dma]
-    scratch += [dma((24,)), dma((24,)), dma((18,)), dma((18,)), dma((18,)), dma((18,)), dma((12,)), dma((12,))]
+    scratch += [dma((24,)), dma((24,)), dma((72,)), dma((72,)), dma((18,)), dma((18,)), dma((12,)), dma((12,))]
     scratch += [dma, dma, dma]
     depth, color, thumbs = pl.pallas_call(
         kernel,
         out_shape=(
-            jax.ShapeDtypeStruct((2, 16, 128), i32),
-            jax.ShapeDtypeStruct((2, 3, 16, 128), bf16),
-            jax.ShapeDtypeStruct((128, 2, 128), jnp.float32),
+            pltpu.VMEM((2, 16, 128), i32),
+            pltpu.VMEM((2, 3, 16, 128), bf16),
+            pltpu.VMEM((128, 2, 128), jnp.float32),
         ),
         in_specs=[vmem, vmem, vmem, anywhere, anywhere],
         out_specs=(vmem, vmem, vmem),
@@ -311,7 +326,19 @@
         slot_depth[0],
         jnp.swapaxes(slot_color[0], 1, 2),
     )
-    thumbnail = thumbs.reshape(128, 256)[:, :192][owner_map].reshape(128, 3, 64)
+    depth, color, thumbs = pl.pallas_call(
+        settle,
+        out_shape=(
+            jax.ShapeDtypeStruct((2, 16, 128), i32),
+            jax.ShapeDtypeStruct((2, 3, 16, 128), bf16),
+            jax.ShapeDtypeStruct((192, 128), jnp.float32),
+        ),
+        in_specs=[vmem] * 4,
+        out_specs=(vmem, vmem, vmem),
+        compiler_params=pltpu.CompilerParams(vmem_limit_bytes=8 << 20),
+        name="settle",
+    )(owner_map[None], depth, color, thumbs)
+    thumbnail = jnp.transpose(thumbs.reshape(3, 64, 128), (2, 0, 1))
     return depth[None], jnp.swapaxes(color, 1, 2)[None], thumbnail
 
 

time: 47.7 us -> 41.1 us (0.86)
  local copies, waits for them, and re-layouts: 3.64 us -> 0.01 us
  Pallas kernels: 42.6 us -> 40.3 us
  other arithmetic: 0.67 us -> 0 us
    pallas_call x1 -> x2, Pallas kernels: 42.6 us -> 40.3 us  [the longest x1 39.3 us: shards(): pl.pallas_call(kernel, out_shape=(pltpu.VMEM((2, 16, 128), i32), pltpu.VM...]
    unnamed x7 -> x2, local copies, waits for them, and re-layouts: 2.15 us -> 0.01 us
    gather x2 -> x0, local copies, waits for them, and re-layouts: 1.5 us -> none  [shards(): thumbnail = thumbs.reshape(128, 256)[:, :192][owner_map].reshape(128, 3, 64)]
    select_n x1 -> x0, other arithmetic: 0.66 us -> none  [shards(): thumbnail = thumbs.reshape(128, 256)[:, :192][owner_map].reshape(128, 3, 64)]
where the time goes in v2:
time: 41.1 us; the launch traced here: 40.9 us
  Pallas kernels  40.3 us (98%)
  between operations  0.65 us (2%)
    pallas_call x1, Pallas kernels, shards(): pl.pallas_call(kernel, out_shape=(pltpu.VMEM((2, 16, 128), i32), pltpu.VM...  39.3 us
    pallas_call x1, Pallas kernels, shards(): pl.pallas_call(settle, out_shape=(jax.ShapeDtypeStruct((2, 16, 128), i32)...  0.99 us

profile of v2, /device:TPU:1, one launch (start us, length us, event | category | flops | bytes accessed | tf_op | source)
XLA Modules:
  0.0 40.9 jit_solution(4035483820287040179)
XLA Ops:
  0.6 0.0 copy-start
  0.6 39.3 %composite.1 = (s32[2,16,128]{2,1,0:T(8,128)S(1)}, bf16[2,3,16,128]{3,2,1,0:T(8,128)(2,1)S(1)}, f32[128,2,128]{2,1,0:T(2,128)S(1)}) custom-call(s32[1,128]{1,0:T(1,128)} %tiles_ref.1, s32[1,128]{1,0:T(1,128)} %bitcast.12, s32[1,128]{1,0:T(1,128)} %constant.2.clone.place_ref, s32[128,16,128]{2,1,0:T(8,128)} %bitcast.15, bf16[128,3,16,128]{3,2,1,0:T(8,128)(2,1)} %bitcast.14), custom_call_target="tpu_custom_call" | custom-call | tf_op jit(solution)/shard_map/composite/pallas_call | solution.py:310
  39.9 0.0 copy-done
  39.9 1.0 %settle.1 = (s32[2,16,128]{2,1,0:T(8,128)}, bf16[2,3,16,128]{3,2,1,0:T(8,128)(2,1)}, f32[192,128]{1,0:T(8,128)}) custom-call(s32[1,128]{1,0:T(1,128)S(1)} %bitcast.13, s32[2,16,128]{2,1,0:T(8,128)S(1)} %get-tuple-element.9.depth_ref, bf16[2,3,16,128]{3,2,1,0:T(8,128)(2,1)S(1)} %get-tuple-element.10.color_ref, f32[128,2,128]{2,1,0:T(2,128)S(1)} %get-tuple-element.11.thumbs_ref), custom_call_target="tpu_custom_call" | custom-call | tf_op jit(solution)/shard_map/settle/pallas_call | solution.py:329
Async XLA Ops:
  0.6 39.3 %copy-start = (s32[128]{0:T(128)S(1)}, s32[128]{0:T(128)}, u32[]{:S(2)}) copy-start(s32[128]{0:T(128)} %param.6) | copy-start | bytes 1540

commit v3 on v2

--- a/solution.py
+++ b/solution.py
@@ -8,7 +8,7 @@
 
 MESH = pl.DeviceIdType.MESH
 FAR = 1073741824
-ORDER = ((0, 1, 2), (1, 2, 0), (2, 0, 1))
+ORDER = ((0, 2, 1), (1, 2, 0), (2, 0, 1))
 STRIDE = (32, 4, 1)
 COUNT = (3, 3, 2)
 BASE = (0, 48, 96)
@@ -45,7 +45,7 @@
     own_d, own_c, one_d, one_c, out1_d, out1_c, two_d, two_c, out2_d, out2_c,
     last_d, last_c, thumbs,
     load_sem, table_sem, core_send, core_recv, send1, recv1, send2, recv2, send3, recv3,
-    thumb_send, thumb_recv, store_sem,
+    thumb_send, thumb_recv,
 ):
     gx, gy = lax.axis_index("gx"), lax.axis_index("gy")
     core = lax.rem(gx, 2)
@@ -89,24 +89,28 @@
         table_v[c : c + 1, :] = jnp.min(jnp.where(hit, down, 128), axis=0, keepdims=True)
     to_table = pltpu.make_async_copy(table_v, table, table_sem)
     to_table.start()
-    to_table.wait()
-    for load in loads:
-        load.wait()
-    pl.semaphore_wait(barrier, 10)
-
-    def remote(src, dst, sends, recvs, index, target):
-        copy = pltpu.make_async_remote_copy(
-            src_ref=src, dst_ref=dst, send_sem=sends.at[index], recv_sem=recvs.at[index],
-            device_id=target, device_id_type=MESH,
-        )
-        copy.start()
-        return copy
+    with jax.named_scope("load"):
+        to_table.wait()
+        for load in loads:
+            load.wait()
+    with jax.named_scope("greet"):
+        pl.semaphore_wait(barrier, 10)
+
+    def remote(depth, color, sends, recv, target):
+        for part, (src, dst) in enumerate((depth, color)):
+            pltpu.make_async_remote_copy(
+                src_ref=src, dst_ref=dst, send_sem=sends.at[part], recv_sem=recv,
+                device_id=target, device_id_type=MESH,
+            ).start()
+
+    def wait_bytes(ref, count, sem):
+        some = ref.at[pl.ds(0, count)]
+        pltpu.make_async_copy(some, some, sem).wait()
 
     def chunk(stream, off):
         size = 4 * COUNT[stream]
         return BASE[stream] + lax.rem(at[ORDER[stream][1]] + off, 4) * size, size
 
-    core_copies = []
     for n, (stream, off) in enumerate(CHUNKS):
         start, size = chunk(stream, off)
 
@@ -119,17 +123,13 @@
 
         lax.fori_loop(0, size, pack, 0, unroll=4)
         part = pl.ds(start, size)
-        core_copies.append((
-            remote(send_d.at[part], got_d.at[part], core_send, core_recv, 2 * n, partner),
-            remote(send_c.at[part], got_c.at[part], core_send, core_recv, 2 * n + 1, partner),
-        ))
-
-    copies1 = {}
+        remote((send_d.at[part], got_d.at[part]), (send_c.at[part], got_c.at[part]), core_send, core_recv.at[n], partner)
+
     for n, (stream, off) in enumerate(CHUNKS):
         start, size = chunk(stream, off)
         axis, count = ORDER[stream][0], COUNT[stream]
-        for copy in core_copies[n]:
-            copy.wait_recv()
+        with jax.named_scope(f"core_wait#n={n}"):
+            wait_bytes(got_d, size * 5 // 2, core_recv.at[n])
         for step in (1, 3, 2, 0):
             first = start + lax.rem(at[axis] + step, 4) * count
             to_d, to_c = (own_d, own_c) if step else (one_d, one_c)
@@ -148,20 +148,14 @@
             if step:
                 src = pl.ds(first, count)
                 dst = pl.ds(start + at[axis] * count, count)
-                index = 2 * (3 * n + step - 1)
-                copies1[n, step] = (
-                    remote(own_d.at[src], one_d.at[dst], send1, recv1, index, peer(axis, step)),
-                    remote(own_c.at[src], one_c.at[dst], send1, recv1, index + 1, peer(axis, step)),
-                )
-
-    copies2 = {}
+                remote((own_d.at[src], one_d.at[dst]), (own_c.at[src], one_c.at[dst]), send1, recv1.at[n], peer(axis, step))
+
     for n, (stream, off) in enumerate(CHUNKS):
         start, size = chunk(stream, off)
         first, second, third = ORDER[stream]
         count, base = COUNT[stream], BASE[stream] // 4
-        for step in (1, 3, 2):
-            for copy in copies1[n, step]:
-                copy.wait_recv()
+        with jax.named_scope(f"wait1#n={n}"):
+            wait_bytes(one_c, 5 * count, recv1.at[n])
         rest = at[second] * STRIDE[second] + at[third] * STRIDE[third]
         if off:
             to_d, to_c, into = out1_d, out1_c, base + (off - 1) * count
@@ -193,11 +187,7 @@
         if off:
             src = pl.ds(into, count)
             dst = pl.ds(base + at[second] * count, count)
-            index = 2 * (3 * stream + off - 1)
-            copies2[stream, off] = (
-                remote(out1_d.at[src], two_d.at[dst], send2, recv2, index, peer(second, off)),
-                remote(out1_c.at[src], two_c.at[dst], send2, recv2, index + 1, peer(second, off)),
-            )
+            remote((out1_d.at[src], two_d.at[dst]), (out1_c.at[src], two_c.at[dst]), send2, recv2.at[stream], peer(second, off))
 
     def closer(depth, color, best, kept):
         tag, old = color[3].astype(jnp.float32), kept[3].astype(jnp.float32)
@@ -206,9 +196,8 @@
 
     for stream in range(3):
         count, base = COUNT[stream], BASE[stream] // 4
-        for off in (1, 2, 3):
-            for copy in copies2[stream, off]:
-                copy.wait_recv()
+        with jax.named_scope(f"wait2#s={stream}"):
+            wait_bytes(two_d, 9 * count, recv2.at[stream])
         for t in range(count):
             best, kept = two_d[base + t], two_c[base + t]
             for src in (1, 2, 3):
@@ -218,33 +207,32 @@
             out2_d[k] = best
             out2_c[k] = kept
 
-    x, y, z = at
-    mine = lax.rem(x + y + z, 4)
-    copies3 = {}
+    def is_third(axis, group, half):
+        found = False
+        for stream in range(3):
+            if ORDER[stream][2] == axis:
+                for c, h in zip(CLASS[stream], HALF[stream]):
+                    if h == half:
+                        found = found | (group == c)
+        return found
+
+    mine = lax.rem(at[0] + at[1] + at[2], 4)
     for off in (1, 2, 3):
         theirs = lax.rem(mine + off, 4)
         for half in range(2):
-            along_z = (theirs == 0) | ((theirs == 3) & (half == 0))
-            along_y = theirs == 2
-            along_x = (theirs == 1) | ((theirs == 3) & (half == 1))
-            target = device(
-                lax.rem(x + jnp.where(along_x, off, 0), 4),
-                lax.rem(y + jnp.where(along_y, off, 0), 4),
-                lax.rem(z + jnp.where(along_z, off, 0), 4),
-            )
+            target = device(*(
+                lax.rem(a + jnp.where(is_third(axis, theirs, half), off, 0), 4) for axis, a in enumerate(at)
+            ))
             k = 2 * theirs + half
             slot = 3 * half + off - 1
-            copies3[half, off] = (
-                remote(out2_d.at[k], last_d.at[slot], send3, recv3, 2 * slot, target),
-                remote(out2_c.at[k], last_c.at[slot], send3, recv3, 2 * slot + 1, target),
-            )
-
+            remote((out2_d.at[k], last_d.at[slot]), (out2_c.at[k], last_c.at[slot]), send3, recv3, target)
+
+    with jax.named_scope("wait3"):
+        wait_bytes(one_d, 18, recv3)
     sums = []
     for half in range(2):
         best, kept = out2_d[2 * mine + half], out2_c[2 * mine + half]
         for off in (1, 2, 3):
-            for copy in copies3[half, off]:
-                copy.wait_recv()
             slot = 3 * half + off - 1
             best, kept = closer(last_d[slot], last_c[slot], best, kept)
         depth_out[half] = best + FAR
@@ -271,13 +259,15 @@
                     src_ref=thumbs.at[me], dst_ref=thumbs.at[me], send_sem=thumb_send, recv_sem=thumb_recv,
                     device_id=(across[other][dx], along[dy][dz]), device_id_type=MESH,
                 ).start()
-    for group_of in (core_copies, copies1.values(), copies2.values(), copies3.values()):
-        for pair in group_of:
-            for copy in pair:
-                copy.wait_send()
-    most = thumbs.at[pl.ds(0, 127)]
-    pltpu.make_async_copy(most, most, thumb_recv).wait()
-    pltpu.make_async_copy(most, most, thumb_send).wait()
+    for sends, depth_ref, color_ref, count in (
+        (core_send, send_d, send_c, 128), (send1, own_d, own_c, 96),
+        (send2, two_d, two_c, 24), (send3, last_d, last_c, 6),
+    ):
+        wait_bytes(depth_ref, count, sends.at[0])
+        wait_bytes(color_ref, count, sends.at[1])
+    with jax.named_scope("thumb_wait"):
+        wait_bytes(thumbs, 127, thumb_recv)
+    wait_bytes(thumbs, 127, thumb_send)
     thumbs_out[...] = thumbs[...]
 
 
@@ -305,8 +295,8 @@
     for tiles, channels in ((128, 3), (128, 3), (128, 3), (128, 3), (32, 4), (32, 4), (8, 4), (6, 4)):
         scratch += [pltpu.VMEM((tiles, 16, 128), i32), pltpu.VMEM((tiles, channels, 16, 128), bf16)]
     scratch += [pltpu.VMEM((128, 2, 128), jnp.float32), dma((2,)), dma]
-    scratch += [dma((24,)), dma((24,)), dma((72,)), dma((72,)), dma((18,)), dma((18,)), dma((12,)), dma((12,))]
-    scratch += [dma, dma, dma]
+    scratch += [dma((2,)), dma((12,)), dma((2,)), dma((12,)), dma((2,)), dma((3,)), dma((2,)), dma]
+    scratch += [dma, dma]
     depth, color, thumbs = pl.pallas_call(
         kernel,
         out_shape=(

time: 41.1 us -> 39.9 us (0.971)
  Pallas kernels: 40.3 us -> 39 us
    pallas_call x1, Pallas kernels: 39.3 us -> 38.1 us  [shards(): pl.pallas_call(kernel, out_shape=(pltpu.VMEM((2, 16, 128), i32), pltpu.VM...]
where the time goes in v3:
time: 39.9 us; the launch traced here: 39.7 us
  Pallas kernels  39 us (98%)
  between operations  0.65 us (2%)
    pallas_call x1, Pallas kernels, shards(): pl.pallas_call(kernel, out_shape=(pltpu.VMEM((2, 16, 128), i32), pltpu.VM...  38.1 us
    pallas_call x1, Pallas kernels, shards(): pl.pallas_call(settle, out_shape=(jax.ShapeDtypeStruct((2, 16, 128), i32)...  0.99 us

profile of v3, /device:TPU:1, one launch (start us, length us, event | category | flops | bytes accessed | tf_op | source)
XLA Modules:
  0.0 39.7 jit_solution(15264426952786548497)
XLA Ops:
  0.6 0.0 copy-start
  0.6 38.1 %composite.1 = (s32[2,16,128]{2,1,0:T(8,128)S(1)}, bf16[2,3,16,128]{3,2,1,0:T(8,128)(2,1)S(1)}, f32[128,2,128]{2,1,0:T(2,128)S(1)}) custom-call(s32[1,128]{1,0:T(1,128)} %tiles_ref.1, s32[1,128]{1,0:T(1,128)} %bitcast.12, s32[1,128]{1,0:T(1,128)} %constant.2.clone.place_ref, s32[128,16,128]{2,1,0:T(8,128)} %bitcast.15, bf16[128,3,16,128]{3,2,1,0:T(8,128)(2,1)} %bitcast.14), custom_call_target="tpu_custom_call" | custom-call | tf_op jit(solution)/shard_map/composite/pallas_call | solution.py:300
  38.7 0.0 copy-done
  38.7 1.0 %settle.1 = (s32[2,16,128]{2,1,0:T(8,128)}, bf16[2,3,16,128]{3,2,1,0:T(8,128)(2,1)}, f32[192,128]{1,0:T(8,128)}) custom-call(s32[1,128]{1,0:T(1,128)S(1)} %bitcast.13, s32[2,16,128]{2,1,0:T(8,128)S(1)} %get-tuple-element.9.depth_ref, bf16[2,3,16,128]{3,2,1,0:T(8,128)(2,1)S(1)} %get-tuple-element.10.color_ref, f32[128,2,128]{2,1,0:T(2,128)S(1)} %get-tuple-element.11.thumbs_ref), custom_call_target="tpu_custom_call" | custom-call | tf_op jit(solution)/shard_map/settle/pallas_call | solution.py:319
Async XLA Ops:
  0.6 38.1 %copy-start = (s32[128]{0:T(128)S(1)}, s32[128]{0:T(128)}, u32[]{:S(2)}) copy-start(s32[128]{0:T(128)} %param.6) | copy-start | bytes 1540

commit v4 on v3

--- a/solution.py
+++ b/solution.py
@@ -8,13 +8,15 @@
 
 MESH = pl.DeviceIdType.MESH
 FAR = 1073741824
-ORDER = ((0, 2, 1), (1, 2, 0), (2, 0, 1))
+ORDER = ((0, 1, 2), (1, 2, 0), (2, 0, 1))
 STRIDE = (32, 4, 1)
 COUNT = (3, 3, 2)
 BASE = (0, 48, 96)
 CLASS = ((0, 0, 3), (1, 1, 3), (2, 2))
 HALF = ((0, 1, 0), (0, 1, 1), (0, 1))
 CHUNKS = tuple((stream, off) for off in (1, 3, 2, 0) for stream in range(3))
+PLAIN = (1, 2)
+STARTS = tuple(sum(4 * COUNT[s] for s, _ in CHUNKS[:n]) for n in range(12))
 FAR_FIRST = sorted(np.ndindex(4, 4, 4), key=lambda d: -sum(min(a, 4 - a) for a in d))
 
 
@@ -42,9 +44,9 @@
     tiles_ref, owner_ref, place_ref, depth_hbm, color_hbm,
     depth_out, color_out, thumbs_out,
     in_d, in_c, table_v, table, send_d, send_c, got_d, got_c,
-    own_d, own_c, one_d, one_c, out1_d, out1_c, two_d, two_c, out2_d, out2_c,
+    own_d, own_c, one_d, one_c, mid_d, mid_c, pass_d, pass_c, met_d, met_c, out1_d, out1_c, two_d, two_c, out2_d, out2_c,
     last_d, last_c, thumbs,
-    load_sem, table_sem, core_send, core_recv, send1, recv1, send2, recv2, send3, recv3,
+    load_sem, table_sem, core_send, core_recv, send1, recv1, send1b, recv1b, send2, recv2, send3, recv3,
     thumb_send, thumb_recv,
 ):
     gx, gy = lax.axis_index("gx"), lax.axis_index("gy")
@@ -125,74 +127,109 @@
         part = pl.ds(start, size)
         remote((send_d.at[part], got_d.at[part]), (send_c.at[part], got_c.at[part]), core_send, core_recv.at[n], partner)
 
+    def others(axis):
+        c = at[axis]
+        return c, c + 1 - 2 * lax.rem(c, 2), lax.rem(c + 2, 4), 3 - c
+
+    def seat(axis, place):
+        return device(*(place if k == axis else a for k, a in enumerate(at)))
+
     for n, (stream, off) in enumerate(CHUNKS):
         start, size = chunk(stream, off)
         axis, count = ORDER[stream][0], COUNT[stream]
         with jax.named_scope(f"core_wait#n={n}"):
             wait_bytes(got_d, size * 5 // 2, core_recv.at[n])
-        for step in (1, 3, 2, 0):
-            first = start + lax.rem(at[axis] + step, 4) * count
-            to_d, to_c = (own_d, own_c) if step else (one_d, one_c)
+        sent = (1, 2) if off in PLAIN else (2, 3)
+        places = others(axis)
+        for rel in sent + tuple(r for r in range(4) if r not in sent):
+            first, into = start + places[rel] * count, STARTS[n] + rel * count
 
             def meet(t, carry):
-                q = first + t
-                slot = table[core, q]
+                slot = table[core, first + t]
                 mine = (in_d[slot] - FAR) * 2 + core
-                other = (got_d[q] - FAR) * 2 + (1 - core)
+                other = (got_d[first + t] - FAR) * 2 + (1 - core)
                 nearer = other < mine
-                to_d[q] = jnp.where(nearer, other, mine)
-                to_c[q] = pick(nearer, got_c[q], in_c[slot])
+                own_d[into + t] = jnp.where(nearer, other, mine)
+                own_c[into + t] = pick(nearer, got_c[first + t], in_c[slot])
                 return carry
 
             lax.fori_loop(0, count, meet, 0, unroll=True)
-            if step:
-                src = pl.ds(first, count)
-                dst = pl.ds(start + at[axis] * count, count)
-                remote((own_d.at[src], one_d.at[dst]), (own_c.at[src], one_c.at[dst]), send1, recv1.at[n], peer(axis, step))
-
-    for n, (stream, off) in enumerate(CHUNKS):
-        start, size = chunk(stream, off)
-        first, second, third = ORDER[stream]
-        count, base = COUNT[stream], BASE[stream] // 4
-        with jax.named_scope(f"wait1#n={n}"):
-            wait_bytes(one_c, 5 * count, recv1.at[n])
-        rest = at[second] * STRIDE[second] + at[third] * STRIDE[third]
-        if off:
-            to_d, to_c, into = out1_d, out1_c, base + (off - 1) * count
-        else:
-            to_d, to_c, into = two_d, two_c, base + at[second] * count
-
-        def join(t, carry):
-            key = tag = color = best = None
-            for src in range(4):
-                q = start + src * count + t
-                k = one_d[q]
-                depth = lax.shift_right_arithmetic(k, 1)
-                order = depth if first == 0 else k
-                rank = rest + src * STRIDE[first] + (k & 1) * 16
-                if src == 0:
-                    key, best, tag, color = order, depth, rank, one_c[q]
-                else:
-                    nearer = order < key
-                    key = jnp.where(nearer, order, key)
-                    best = jnp.where(nearer, depth, best)
-                    tag = jnp.where(nearer, rank, tag)
-                    color = pick(nearer, one_c[q], color)
-            to_d[into + t] = best
-            to_c[into + t, 0:3] = color
-            to_c[into + t, 3] = tag.astype(jnp.float32).astype(jnp.bfloat16)
-            return carry
-
-        lax.fori_loop(0, count, join, 0)
-        if off:
-            src = pl.ds(into, count)
-            dst = pl.ds(base + at[second] * count, count)
-            remote((out1_d.at[src], two_d.at[dst]), (out1_c.at[src], two_c.at[dst]), send2, recv2.at[stream], peer(second, off))
+            if rel == sent[1]:
+                src = pl.ds(STARTS[n] + sent[0] * count, 2 * count)
+                dst = pl.ds(STARTS[n] // 2, 2 * count)
+                remote(
+                    (own_d.at[src], one_d.at[dst]), (own_c.at[src], one_c.at[dst]),
+                    send1, recv1.at[n], seat(axis, places[1 if off in PLAIN else 3]),
+                )
 
     def closer(depth, color, best, kept):
         tag, old = color[3].astype(jnp.float32), kept[3].astype(jnp.float32)
         nearer = (depth < best) | ((depth == best) & (tag < old))
         return jnp.where(nearer, depth, best), pick(nearer, color, kept)
+
+    def first_join(n):
+        stream, off = CHUNKS[n]
+        first, second, third = ORDER[stream]
+        count = COUNT[stream]
+        places = others(first)
+        near, away = (1, 3) if off in PLAIN else (3, 1)
+        mine, theirs = places[0], places[near]
+        rest = at[second] * STRIDE[second] + at[third] * STRIDE[third]
+        lower = jnp.where(theirs < mine, 1, 0)
+        with jax.named_scope(f"wait1#n={n}"):
+            wait_bytes(one_d, 5 * count, recv1.at[n])
+        for part, rel in enumerate((0, 3) if off in PLAIN else (1, 0)):
+            to_d, to_c = (pass_d, pass_c) if rel else (mid_d, mid_c)
+            base = STARTS[n] // 4
+
+            def join(t, carry):
+                p, q = STARTS[n] + rel * count + t, STARTS[n] // 2 + part * count + t
+                k, other = own_d[p], one_d[q]
+                depth, far_depth = lax.shift_right_arithmetic(k, 1), lax.shift_right_arithmetic(other, 1)
+                nearer = far_depth < depth + lower if first == 0 else other < k + lower
+                own_rank = rest + mine * STRIDE[first] + (k & 1) * 16
+                other_rank = rest + theirs * STRIDE[first] + (other & 1) * 16
+                to_d[base + t] = jnp.where(nearer, far_depth, depth)
+                to_c[base + t, 0:3] = pick(nearer, one_c[q], own_c[p])
+                to_c[base + t, 3] = jnp.where(nearer, other_rank, own_rank).astype(jnp.float32).astype(jnp.bfloat16)
+                return carry
+
+            lax.fori_loop(0, count, join, 0)
+        part = pl.ds(STARTS[n] // 4, count)
+        remote(
+            (pass_d.at[part], met_d.at[part]), (pass_c.at[part], met_c.at[part]),
+            send1b, recv1b.at[n], seat(first, places[away]),
+        )
+
+    def second_join(n):
+        stream, off = CHUNKS[n]
+        second, count = ORDER[stream][1], COUNT[stream]
+        base, into = STARTS[n] // 4, BASE[stream] // 4
+        if off:
+            to_d, to_c, into = out1_d, out1_c, into + (off - 1) * count
+        else:
+            to_d, to_c, into = two_d, two_c, into + at[second] * count
+        with jax.named_scope(f"wait1b#n={n}"):
+            wait_bytes(one_d, 3 * count, recv1b.at[n])
+
+        def join(t, carry):
+            q = base + t
+            to_d[into + t], to_c[into + t] = closer(met_d[q], met_c[q], mid_d[q], mid_c[q])
+            return carry
+
+        lax.fori_loop(0, count, join, 0)
+        if off:
+            src = pl.ds(into, count)
+            dst = pl.ds(BASE[stream] // 4 + at[second] * count, count)
+            remote((out1_d.at[src], two_d.at[dst]), (out1_c.at[src], two_c.at[dst]), send2, recv2.at[stream], peer(second, off))
+
+    for group in range(5):
+        if group < 4:
+            for n in range(3 * group, 3 * group + 3):
+                first_join(n)
+        if group:
+            for n in range(3 * group - 3, 3 * group):
+                second_join(n)
 
     for stream in range(3):
         count, base = COUNT[stream], BASE[stream] // 4
@@ -260,7 +297,7 @@
                     device_id=(across[other][dx], along[dy][dz]), device_id_type=MESH,
                 ).start()
     for sends, depth_ref, color_ref, count in (
-        (core_send, send_d, send_c, 128), (send1, own_d, own_c, 96),
+        (core_send, send_d, send_c, 128), (send1, own_d, own_c, 64), (send1b, met_d, met_c, 32),
         (send2, two_d, two_c, 24), (send3, last_d, last_c, 6),
     ):
         wait_bytes(depth_ref, count, sends.at[0])
@@ -292,10 +329,10 @@
         pltpu.VMEM((129, 16, 128), i32), pltpu.VMEM((129, 3, 16, 128), bf16),
         pltpu.VMEM((2, 128), i32), pltpu.SMEM((2, 128), i32),
     ]
-    for tiles, channels in ((128, 3), (128, 3), (128, 3), (128, 3), (32, 4), (32, 4), (8, 4), (6, 4)):
+    for tiles, channels in ((128, 3), (128, 3), (128, 3), (64, 3), (32, 4), (32, 4), (32, 4), (32, 4), (32, 4), (8, 4), (6, 4)):
         scratch += [pltpu.VMEM((tiles, 16, 128), i32), pltpu.VMEM((tiles, channels, 16, 128), bf16)]
     scratch += [pltpu.VMEM((128, 2, 128), jnp.float32), dma((2,)), dma]
-    scratch += [dma((2,)), dma((12,)), dma((2,)), dma((12,)), dma((2,)), dma((3,)), dma((2,)), dma]
+    scratch += [dma((2,)), dma((12,)), dma((2,)), dma((12,)), dma((2,)), dma((12,)), dma((2,)), dma((3,)), dma((2,)), dma]
     scratch += [dma, dma]
     depth, color, thumbs = pl.pallas_call(
         kernel,

time: 39.9 us -> 42.5 us (1.065)
  Pallas kernels: 39 us -> 41.7 us
    pallas_call x1, Pallas kernels: 38.1 us -> 40.7 us  [shards(): pl.pallas_call(kernel, out_shape=(pltpu.VMEM((2, 16, 128), i32), pltpu.VM...]
where the time goes in v4:
time: 42.5 us; the launch traced here: 42.3 us
  Pallas kernels  41.7 us (98%)
  between operations  0.65 us (2%)
    pallas_call x1, Pallas kernels, shards(): pl.pallas_call(kernel, out_shape=(pltpu.VMEM((2, 16, 128), i32), pltpu.VM...  40.7 us
    pallas_call x1, Pallas kernels, shards(): pl.pallas_call(settle, out_shape=(jax.ShapeDtypeStruct((2, 16, 128), i32)...  0.99 us

profile of v4, /device:TPU:1, one launch (start us, length us, event | category | flops | bytes accessed | tf_op | source)
XLA Modules:
  0.0 42.3 jit_solution(3378859618067080346)
XLA Ops:
  0.6 0.0 copy-start
  0.6 40.7 %composite.1 = (s32[2,16,128]{2,1,0:T(8,128)S(1)}, bf16[2,3,16,128]{3,2,1,0:T(8,128)(2,1)S(1)}, f32[128,2,128]{2,1,0:T(2,128)S(1)}) custom-call(s32[1,128]{1,0:T(1,128)} %tiles_ref.1, s32[1,128]{1,0:T(1,128)} %bitcast.12, s32[1,128]{1,0:T(1,128)} %constant.2.clone.place_ref, s32[128,16,128]{2,1,0:T(8,128)} %bitcast.15, bf16[128,3,16,128]{3,2,1,0:T(8,128)(2,1)} %bitcast.14), custom_call_target="tpu_custom_call" | custom-call | tf_op jit(solution)/shard_map/composite/pallas_call | solution.py:337
  41.3 0.0 copy-done
  41.3 1.0 %settle.1 = (s32[2,16,128]{2,1,0:T(8,128)}, bf16[2,3,16,128]{3,2,1,0:T(8,128)(2,1)}, f32[192,128]{1,0:T(8,128)}) custom-call(s32[1,128]{1,0:T(1,128)S(1)} %bitcast.13, s32[2,16,128]{2,1,0:T(8,128)S(1)} %get-tuple-element.9.depth_ref, bf16[2,3,16,128]{3,2,1,0:T(8,128)(2,1)S(1)} %get-tuple-element.10.color_ref, f32[128,2,128]{2,1,0:T(2,128)S(1)} %get-tuple-element.11.thumbs_ref), custom_call_target="tpu_custom_call" | custom-call | tf_op jit(solution)/shard_map/settle/pallas_call | solution.py:356
Async XLA Ops:
  0.6 40.7 %copy-start = (s32[128]{0:T(128)S(1)}, s32[128]{0:T(128)}, u32[]{:S(2)}) copy-start(s32[128]{0:T(128)} %param.6) | copy-start | bytes 1540

commit v5 on v4

--- a/solution.py
+++ b/solution.py
@@ -14,8 +14,8 @@
 BASE = (0, 48, 96)
 CLASS = ((0, 0, 3), (1, 1, 3), (2, 2))
 HALF = ((0, 1, 0), (0, 1, 1), (0, 1))
-CHUNKS = tuple((stream, off) for off in (1, 3, 2, 0) for stream in range(3))
-PLAIN = (1, 2)
+CHUNKS = tuple((stream, off) for off in (2, 1, 3, 0) for stream in range(3))
+PLAIN = (2, 3)
 STARTS = tuple(sum(4 * COUNT[s] for s, _ in CHUNKS[:n]) for n in range(12))
 FAR_FIRST = sorted(np.ndindex(4, 4, 4), key=lambda d: -sum(min(a, 4 - a) for a in d))
 
@@ -223,13 +223,10 @@
             dst = pl.ds(BASE[stream] // 4 + at[second] * count, count)
             remote((out1_d.at[src], two_d.at[dst]), (out1_c.at[src], two_c.at[dst]), send2, recv2.at[stream], peer(second, off))
 
-    for group in range(5):
-        if group < 4:
-            for n in range(3 * group, 3 * group + 3):
-                first_join(n)
-        if group:
-            for n in range(3 * group - 3, 3 * group):
-                second_join(n)
+    for n in range(12):
+        first_join(n)
+    for n in range(12):
+        second_join(n)
 
     for stream in range(3):
         count, base = COUNT[stream], BASE[stream] // 4
@@ -254,7 +251,7 @@
         return found
 
     mine = lax.rem(at[0] + at[1] + at[2], 4)
-    for off in (1, 2, 3):
+    for off in (2, 1, 3):
         theirs = lax.rem(mine + off, 4)
         for half in range(2):
             target = device(*(

time: 42.5 us -> 39.3 us (0.925)
  Pallas kernels: 41.7 us -> 38.4 us
    pallas_call x1, Pallas kernels: 40.7 us -> 37.5 us  [shards(): pl.pallas_call(kernel, out_shape=(pltpu.VMEM((2, 16, 128), i32), pltpu.VM...]
where the time goes in v5:
time: 39.3 us; the launch traced here: 39.1 us
  Pallas kernels  38.4 us (98%)
  between operations  0.65 us (2%)
    pallas_call x1, Pallas kernels, shards(): pl.pallas_call(kernel, out_shape=(pltpu.VMEM((2, 16, 128), i32), pltpu.VM...  37.5 us
    pallas_call x1, Pallas kernels, shards(): pl.pallas_call(settle, out_shape=(jax.ShapeDtypeStruct((2, 16, 128), i32)...  0.99 us

profile of v5, /device:TPU:1, one launch (start us, length us, event | category | flops | bytes accessed | tf_op | source)
XLA Modules:
  0.0 39.1 jit_solution(8942402293395711232)
XLA Ops:
  0.6 0.0 copy-start
  0.6 37.5 %composite.1 = (s32[2,16,128]{2,1,0:T(8,128)S(1)}, bf16[2,3,16,128]{3,2,1,0:T(8,128)(2,1)S(1)}, f32[128,2,128]{2,1,0:T(2,128)S(1)}) custom-call(s32[1,128]{1,0:T(1,128)} %tiles_ref.1, s32[1,128]{1,0:T(1,128)} %bitcast.12, s32[1,128]{1,0:T(1,128)} %constant.2.clone.place_ref, s32[128,16,128]{2,1,0:T(8,128)} %bitcast.15, bf16[128,3,16,128]{3,2,1,0:T(8,128)(2,1)} %bitcast.14), custom_call_target="tpu_custom_call" | custom-call | tf_op jit(solution)/shard_map/composite/pallas_call | solution.py:334
  38.1 0.0 copy-done
  38.1 1.0 %settle.1 = (s32[2,16,128]{2,1,0:T(8,128)}, bf16[2,3,16,128]{3,2,1,0:T(8,128)(2,1)}, f32[192,128]{1,0:T(8,128)}) custom-call(s32[1,128]{1,0:T(1,128)S(1)} %bitcast.13, s32[2,16,128]{2,1,0:T(8,128)S(1)} %get-tuple-element.9.depth_ref, bf16[2,3,16,128]{3,2,1,0:T(8,128)(2,1)S(1)} %get-tuple-element.10.color_ref, f32[128,2,128]{2,1,0:T(2,128)S(1)} %get-tuple-element.11.thumbs_ref), custom_call_target="tpu_custom_call" | custom-call | tf_op jit(solution)/shard_map/settle/pallas_call | solution.py:353
Async XLA Ops:
  0.6 37.5 %copy-start = (s32[128]{0:T(128)S(1)}, s32[128]{0:T(128)}, u32[]{:S(2)}) copy-start(s32[128]{0:T(128)} %param.6) | copy-start | bytes 1540

commit v6 on v5

--- a/solution.py
+++ b/solution.py
@@ -12,8 +12,8 @@
 STRIDE = (32, 4, 1)
 COUNT = (3, 3, 2)
 BASE = (0, 48, 96)
-CLASS = ((0, 0, 3), (1, 1, 3), (2, 2))
-HALF = ((0, 1, 0), (0, 1, 1), (0, 1))
+CLASS = ((0, 2, 3), (0, 1, 3), (1, 2))
+HALF = ((0, 1, 0), (1, 0, 1), (1, 0))
 CHUNKS = tuple((stream, off) for off in (2, 1, 3, 0) for stream in range(3))
 PLAIN = (2, 3)
 STARTS = tuple(sum(4 * COUNT[s] for s, _ in CHUNKS[:n]) for n in range(12))
@@ -228,7 +228,8 @@
     for n in range(12):
         second_join(n)
 
-    for stream in range(3):
+    mine = lax.rem(at[0] + at[1] + at[2], 4)
+    for stream in (2, 1, 0):
         count, base = COUNT[stream], BASE[stream] // 4
         with jax.named_scope(f"wait2#s={stream}"):
             wait_bytes(two_d, 9 * count, recv2.at[stream])
@@ -237,29 +238,19 @@
             for src in (1, 2, 3):
                 q = base + src * count + t
                 best, kept = closer(two_d[q], two_c[q], best, kept)
-            k = 2 * CLASS[stream][t] + HALF[stream][t]
+            group, half = CLASS[stream][t], HALF[stream][t]
+            k = 2 * group + half
             out2_d[k] = best
             out2_c[k] = kept
-
-    def is_third(axis, group, half):
-        found = False
-        for stream in range(3):
-            if ORDER[stream][2] == axis:
-                for c, h in zip(CLASS[stream], HALF[stream]):
-                    if h == half:
-                        found = found | (group == c)
-        return found
-
-    mine = lax.rem(at[0] + at[1] + at[2], 4)
-    for off in (2, 1, 3):
-        theirs = lax.rem(mine + off, 4)
-        for half in range(2):
-            target = device(*(
-                lax.rem(a + jnp.where(is_third(axis, theirs, half), off, 0), 4) for axis, a in enumerate(at)
-            ))
-            k = 2 * theirs + half
-            slot = 3 * half + off - 1
-            remote((out2_d.at[k], last_d.at[slot]), (out2_c.at[k], last_c.at[slot]), send3, recv3, target)
+            off = lax.rem(group - mine + 4, 4)
+
+            @pl.when(off != 0)
+            def send():
+                slot = 3 * half + off - 1
+                remote(
+                    (out2_d.at[k], last_d.at[slot]), (out2_c.at[k], last_c.at[slot]),
+                    send3, recv3, peer(ORDER[stream][2], off),
+                )
 
     with jax.named_scope("wait3"):
         wait_bytes(one_d, 18, recv3)

time: 39.3 us -> 38.4 us (0.977)
  Pallas kernels: 38.4 us -> 37.6 us
    pallas_call x1, Pallas kernels: 37.5 us -> 36.6 us  [shards(): pl.pallas_call(kernel, out_shape=(pltpu.VMEM((2, 16, 128), i32), pltpu.VM...]
where the time goes in v6:
time: 38.4 us; the launch traced here: 38.3 us
  Pallas kernels  37.6 us (98%)
  between operations  0.65 us (2%)
    pallas_call x1, Pallas kernels, shards(): pl.pallas_call(kernel, out_shape=(pltpu.VMEM((2, 16, 128), i32), pltpu.VM...  36.6 us
    pallas_call x1, Pallas kernels, shards(): pl.pallas_call(settle, out_shape=(jax.ShapeDtypeStruct((2, 16, 128), i32)...  0.99 us

profile of v6, /device:TPU:1, one launch (start us, length us, event | category | flops | bytes accessed | tf_op | source)
XLA Modules:
  0.0 38.3 jit_solution(276130299205169170)
XLA Ops:
  0.6 0.0 copy-start
  0.6 36.6 %composite.1 = (s32[2,16,128]{2,1,0:T(8,128)S(1)}, bf16[2,3,16,128]{3,2,1,0:T(8,128)(2,1)S(1)}, f32[128,2,128]{2,1,0:T(2,128)S(1)}) custom-call(s32[1,128]{1,0:T(1,128)} %tiles_ref.1, s32[1,128]{1,0:T(1,128)} %bitcast.12, s32[1,128]{1,0:T(1,128)} %constant.2.clone.place_ref, s32[128,16,128]{2,1,0:T(8,128)} %bitcast.15, bf16[128,3,16,128]{3,2,1,0:T(8,128)(2,1)} %bitcast.14), custom_call_target="tpu_custom_call" | custom-call | tf_op jit(solution)/shard_map/composite/pallas_call | solution.py:325
  37.3 0.0 copy-done
  37.3 1.0 %settle.1 = (s32[2,16,128]{2,1,0:T(8,128)}, bf16[2,3,16,128]{3,2,1,0:T(8,128)(2,1)}, f32[192,128]{1,0:T(8,128)}) custom-call(s32[1,128]{1,0:T(1,128)S(1)} %bitcast.13, s32[2,16,128]{2,1,0:T(8,128)S(1)} %get-tuple-element.9.depth_ref, bf16[2,3,16,128]{3,2,1,0:T(8,128)(2,1)S(1)} %get-tuple-element.10.color_ref, f32[128,2,128]{2,1,0:T(2,128)S(1)} %get-tuple-element.11.thumbs_ref), custom_call_target="tpu_custom_call" | custom-call | tf_op jit(solution)/shard_map/settle/pallas_call | solution.py:344
Async XLA Ops:
  0.6 36.6 %copy-start = (s32[128]{0:T(128)S(1)}, s32[128]{0:T(128)}, u32[]{:S(2)}) copy-start(s32[128]{0:T(128)} %param.6) | copy-start | bytes 1540

commit v7 on v6

--- a/solution.py
+++ b/solution.py
@@ -16,7 +16,23 @@
 HALF = ((0, 1, 0), (1, 0, 1), (1, 0))
 CHUNKS = tuple((stream, off) for off in (2, 1, 3, 0) for stream in range(3))
 PLAIN = (2, 3)
-STARTS = tuple(sum(4 * COUNT[s] for s, _ in CHUNKS[:n]) for n in range(12))
+SINGLE = (2, 1, 3)
+
+
+def parts():
+    out = []
+    for first in range(0, 12, 3):
+        chunks = range(first, first + 3)
+        if CHUNKS[first][1] in SINGLE:
+            out += [(n, t, 1) for t in range(3) for n in chunks if t < COUNT[CHUNKS[n][0]]]
+        else:
+            out += [(n, 0, COUNT[CHUNKS[n][0]]) for n in chunks]
+    return tuple(out)
+
+
+PARTS = parts()
+STARTS = tuple(sum(4 * count for _, _, count in PARTS[:m]) for m in range(len(PARTS)))
+KEPT = len(PARTS) - 3
 FAR_FIRST = sorted(np.ndindex(4, 4, 4), key=lambda d: -sum(min(a, 4 - a) for a in d))
 
 
@@ -44,7 +60,7 @@
     tiles_ref, owner_ref, place_ref, depth_hbm, color_hbm,
     depth_out, color_out, thumbs_out,
     in_d, in_c, table_v, table, send_d, send_c, got_d, got_c,
-    own_d, own_c, one_d, one_c, mid_d, mid_c, pass_d, pass_c, met_d, met_c, out1_d, out1_c, two_d, two_c, out2_d, out2_c,
+    own_d, own_c, one_d, one_c, mid_d, mid_c, pass_d, pass_c, met_d, met_c, keep_d, keep_c, out1_d, out1_c, two_d, two_c, out2_d, out2_c,
     last_d, last_c, thumbs,
     load_sem, table_sem, core_send, core_recv, send1, recv1, send1b, recv1b, send2, recv2, send3, recv3,
     thumb_send, thumb_recv,
@@ -134,15 +150,36 @@
     def seat(axis, place):
         return device(*(place if k == axis else a for k, a in enumerate(at)))
 
-    for n, (stream, off) in enumerate(CHUNKS):
-        start, size = chunk(stream, off)
-        axis, count = ORDER[stream][0], COUNT[stream]
-        with jax.named_scope(f"core_wait#n={n}"):
-            wait_bytes(got_d, size * 5 // 2, core_recv.at[n])
-        sent = (1, 2) if off in PLAIN else (2, 3)
-        places = others(axis)
-        for rel in sent + tuple(r for r in range(4) if r not in sent):
-            first, into = start + places[rel] * count, STARTS[n] + rel * count
+    def piece(m):
+        n, skip, count = PARTS[m]
+        return *CHUNKS[n], skip, count
+
+    def first_send(n):
+        stream, off, _, count = piece(n)
+        axis = ORDER[stream][0]
+        near, skip = (1, 1) if off in PLAIN else (3, 2)
+        src = pl.ds(STARTS[n] + skip * count, 2 * count)
+        dst = pl.ds(STARTS[n] // 2, 2 * count)
+        remote(
+            (own_d.at[src], one_d.at[dst]), (own_c.at[src], one_c.at[dst]),
+            send1, recv1.at[n], seat(axis, others(axis)[near]),
+        )
+
+    def keep_send(n, rel):
+        stream, off, _, count = piece(n)
+        axis = ORDER[stream][0]
+        src = pl.ds(STARTS[n] + rel * count, count)
+        dst = pl.ds((STARTS[n] - STARTS[KEPT]) // 4 * 3 + (rel - 1) * count, count)
+        remote(
+            (own_d.at[src], keep_d.at[dst]), (own_c.at[src], keep_c.at[dst]),
+            send1, recv1.at[n], seat(axis, others(axis)[rel]),
+        )
+
+    def meet_part(m, start):
+        stream, off, skip, count = piece(m)
+        places = others(ORDER[stream][0])
+        for rel in (3, 2, 1, 0) if off not in PLAIN else (1, 2, 3, 0):
+            first, into = start + places[rel] * COUNT[stream] + skip, STARTS[m] + rel * count
 
             def meet(t, carry):
                 slot = table[core, first + t]
@@ -154,13 +191,18 @@
                 return carry
 
             lax.fori_loop(0, count, meet, 0, unroll=True)
-            if rel == sent[1]:
-                src = pl.ds(STARTS[n] + sent[0] * count, 2 * count)
-                dst = pl.ds(STARTS[n] // 2, 2 * count)
-                remote(
-                    (own_d.at[src], one_d.at[dst]), (own_c.at[src], one_c.at[dst]),
-                    send1, recv1.at[n], seat(axis, places[1 if off in PLAIN else 3]),
-                )
+            if rel == 2 and off:
+                first_send(m)
+            if rel == 3 and not off:
+                keep_send(m, rel)
+
+    for n, (stream, off) in enumerate(CHUNKS):
+        start, size = chunk(stream, off)
+        with jax.named_scope(f"core_wait#n={n}"):
+            wait_bytes(got_d, size * 5 // 2, core_recv.at[n])
+        for m in range(len(PARTS)):
+            if PARTS[m][0] == n:
+                meet_part(m, start)
 
     def closer(depth, color, best, kept):
         tag, old = color[3].astype(jnp.float32), kept[3].astype(jnp.float32)
@@ -168,9 +210,8 @@
         return jnp.where(nearer, depth, best), pick(nearer, color, kept)
 
     def first_join(n):
-        stream, off = CHUNKS[n]
+        stream, off, _, count = piece(n)
         first, second, third = ORDER[stream]
-        count = COUNT[stream]
         places = others(first)
         near, away = (1, 3) if off in PLAIN else (3, 1)
         mine, theirs = places[0], places[near]
@@ -202,31 +243,62 @@
         )
 
     def second_join(n):
-        stream, off = CHUNKS[n]
-        second, count = ORDER[stream][1], COUNT[stream]
-        base, into = STARTS[n] // 4, BASE[stream] // 4
-        if off:
-            to_d, to_c, into = out1_d, out1_c, into + (off - 1) * count
-        else:
-            to_d, to_c, into = two_d, two_c, into + at[second] * count
+        stream, off, skip, count = piece(n)
+        second = ORDER[stream][1]
+        base, into = STARTS[n] // 4, BASE[stream] // 4 + (off - 1) * COUNT[stream] + skip
         with jax.named_scope(f"wait1b#n={n}"):
             wait_bytes(one_d, 3 * count, recv1b.at[n])
 
         def join(t, carry):
             q = base + t
-            to_d[into + t], to_c[into + t] = closer(met_d[q], met_c[q], mid_d[q], mid_c[q])
+            out1_d[into + t], out1_c[into + t] = closer(met_d[q], met_c[q], mid_d[q], mid_c[q])
             return carry
 
         lax.fori_loop(0, count, join, 0)
-        if off:
-            src = pl.ds(into, count)
-            dst = pl.ds(BASE[stream] // 4 + at[second] * count, count)
-            remote((out1_d.at[src], two_d.at[dst]), (out1_c.at[src], two_c.at[dst]), send2, recv2.at[stream], peer(second, off))
-
-    for n in range(12):
-        first_join(n)
-    for n in range(12):
-        second_join(n)
+        src = pl.ds(into, count)
+        dst = pl.ds(BASE[stream] // 4 + at[second] * COUNT[stream] + skip, count)
+        remote((out1_d.at[src], two_d.at[dst]), (out1_c.at[src], two_c.at[dst]), send2, recv2.at[stream], peer(second, off))
+
+    def keep_join(n):
+        stream, off, _, count = piece(n)
+        first, second, third = ORDER[stream]
+        base = (STARTS[n] - STARTS[KEPT]) // 4 * 3
+        into = BASE[stream] // 4 + at[second] * count
+        places = others(first)
+        rest = at[second] * STRIDE[second] + at[third] * STRIDE[third]
+        with jax.named_scope(f"keep_wait#n={n}"):
+            wait_bytes(own_c, 5 * count, recv1.at[n])
+
+        def join(t, carry):
+            best = tag = color = None
+            for rel in range(4):
+                q = base + (rel - 1) * count + t
+                k, new = (keep_d[q], keep_c[q]) if rel else (own_d[STARTS[n] + t], own_c[STARTS[n] + t])
+                depth = lax.shift_right_arithmetic(k, 1)
+                rank = rest + places[rel] * STRIDE[first] + (k & 1) * 16
+                if rel == 0:
+                    best, tag, color = depth, rank, new
+                else:
+                    nearer = (depth < best) | ((depth == best) & (rank < tag))
+                    best, tag = jnp.where(nearer, depth, best), jnp.where(nearer, rank, tag)
+                    color = pick(nearer, new, color)
+            two_d[into + t] = best
+            two_c[into + t, 0:3] = color
+            two_c[into + t, 3] = tag.astype(jnp.float32).astype(jnp.bfloat16)
+            return carry
+
+        lax.fori_loop(0, count, join, 0)
+
+    last_of = {PARTS[m][0]: m for m in range(KEPT)}
+    for m in range(KEPT):
+        first_join(m)
+        for n in range(6):
+            if last_of[n] == m:
+                keep_send(KEPT + n % 3, 2 - n // 3)
+    for m in range(KEPT):
+        second_join(m)
+    for m in range(KEPT, len(PARTS)):
+        keep_join(m)
 
     mine = lax.rem(at[0] + at[1] + at[2], 4)
     for stream in (2, 1, 0):
@@ -285,7 +357,7 @@
                     device_id=(across[other][dx], along[dy][dz]), device_id_type=MESH,
                 ).start()
     for sends, depth_ref, color_ref, count in (
-        (core_send, send_d, send_c, 128), (send1, own_d, own_c, 64), (send1b, met_d, met_c, 32),
+        (core_send, send_d, send_c, 128), (send1, own_d, own_c, 72), (send1b, met_d, met_c, 24),
         (send2, two_d, two_c, 24), (send3, last_d, last_c, 6),
     ):
         wait_bytes(depth_ref, count, sends.at[0])
@@ -317,10 +389,10 @@
         pltpu.VMEM((129, 16, 128), i32), pltpu.VMEM((129, 3, 16, 128), bf16),
         pltpu.VMEM((2, 128), i32), pltpu.SMEM((2, 128), i32),
     ]
-    for tiles, channels in ((128, 3), (128, 3), (128, 3), (64, 3), (32, 4), (32, 4), (32, 4), (32, 4), (32, 4), (8, 4), (6, 4)):
+    for tiles, channels in ((128, 3), (128, 3), (128, 3), (48, 3), (24, 4), (24, 4), (24, 4), (24, 3), (32, 4), (32, 4), (8, 4), (6, 4)):
         scratch += [pltpu.VMEM((tiles, 16, 128), i32), pltpu.VMEM((tiles, channels, 16, 128), bf16)]
     scratch += [pltpu.VMEM((128, 2, 128), jnp.float32), dma((2,)), dma]
-    scratch += [dma((2,)), dma((12,)), dma((2,)), dma((12,)), dma((2,)), dma((12,)), dma((2,)), dma((3,)), dma((2,)), dma]
+    scratch += [dma((2,)), dma((12,)), dma((2,)), dma((len(PARTS),)), dma((2,)), dma((KEPT,)), dma((2,)), dma((3,)), dma((2,)), dma]
     scratch += [dma, dma]
     depth, color, thumbs = pl.pallas_call(
         kernel,

time: 38.4 us -> 37.8 us (0.984)
  Pallas kernels: 37.6 us -> 37 us
    pallas_call x1, Pallas kernels: 36.6 us -> 36 us  [shards(): pl.pallas_call(kernel, out_shape=(pltpu.VMEM((2, 16, 128), i32), pltpu.VM...]
where the time goes in v7:
time: 37.8 us; the launch traced here: 37.6 us
  Pallas kernels  37 us (98%)
  between operations  0.65 us (2%)
    pallas_call x1, Pallas kernels, shards(): pl.pallas_call(kernel, out_shape=(pltpu.VMEM((2, 16, 128), i32), pltpu.VM...  36 us
    pallas_call x1, Pallas kernels, shards(): pl.pallas_call(settle, out_shape=(jax.ShapeDtypeStruct((2, 16, 128), i32)...  0.99 us

profile of v7, /device:TPU:1, one launch (start us, length us, event | category | flops | bytes accessed | tf_op | source)
XLA Modules:
  0.0 37.6 jit_solution(1972994829044078763)
XLA Ops:
  0.6 0.0 copy-start
  0.6 36.0 %composite.1 = (s32[2,16,128]{2,1,0:T(8,128)S(1)}, bf16[2,3,16,128]{3,2,1,0:T(8,128)(2,1)S(1)}, f32[128,2,128]{2,1,0:T(2,128)S(1)}) custom-call(s32[1,128]{1,0:T(1,128)} %tiles_ref.1, s32[1,128]{1,0:T(1,128)} %bitcast.12, s32[1,128]{1,0:T(1,128)} %constant.2.clone.place_ref, s32[128,16,128]{2,1,0:T(8,128)} %bitcast.15, bf16[128,3,16,128]{3,2,1,0:T(8,128)(2,1)} %bitcast.14), custom_call_target="tpu_custom_call" | custom-call | tf_op jit(solution)/shard_map/composite/pallas_call | solution.py:397
  36.6 0.0 copy-done
  36.7 1.0 %settle.1 = (s32[2,16,128]{2,1,0:T(8,128)}, bf16[2,3,16,128]{3,2,1,0:T(8,128)(2,1)}, f32[192,128]{1,0:T(8,128)}) custom-call(s32[1,128]{1,0:T(1,128)S(1)} %bitcast.13, s32[2,16,128]{2,1,0:T(8,128)S(1)} %get-tuple-element.9.depth_ref, bf16[2,3,16,128]{3,2,1,0:T(8,128)(2,1)S(1)} %get-tuple-element.10.color_ref, f32[128,2,128]{2,1,0:T(2,128)S(1)} %get-tuple-element.11.thumbs_ref), custom_call_target="tpu_custom_call" | custom-call | tf_op jit(solution)/shard_map/settle/pallas_call | solution.py:416
Async XLA Ops:
  0.6 36.0 %copy-start = (s32[128]{0:T(128)S(1)}, s32[128]{0:T(128)}, u32[]{:S(2)}) copy-start(s32[128]{0:T(128)} %param.6) | copy-start | bytes 1540

commit v8 on v7

--- a/solution.py
+++ b/solution.py
@@ -33,6 +33,8 @@
 PARTS = parts()
 STARTS = tuple(sum(4 * count for _, _, count in PARTS[:m]) for m in range(len(PARTS)))
 KEPT = len(PARTS) - 3
+ROUNDS = sorted({(n // 3, t if n < 9 else 0) for n, t, _ in PARTS})
+ROUND = tuple(ROUNDS.index((n // 3, t)) for n, t, _ in PARTS)
 FAR_FIRST = sorted(np.ndindex(4, 4, 4), key=lambda d: -sum(min(a, 4 - a) for a in d))
 
 
@@ -129,6 +131,9 @@
         size = 4 * COUNT[stream]
         return BASE[stream] + lax.rem(at[ORDER[stream][1]] + off, 4) * size, size
 
+    def slot_of(n):
+        return n if n < 6 else 4 + n // 3
+
     for n, (stream, off) in enumerate(CHUNKS):
         start, size = chunk(stream, off)
 
@@ -141,7 +146,7 @@
 
         lax.fori_loop(0, size, pack, 0, unroll=4)
         part = pl.ds(start, size)
-        remote((send_d.at[part], got_d.at[part]), (send_c.at[part], got_c.at[part]), core_send, core_recv.at[n], partner)
+        remote((send_d.at[part], got_d.at[part]), (send_c.at[part], got_c.at[part]), core_send, core_recv.at[slot_of(n)], partner)
 
     def others(axis):
         c = at[axis]
@@ -149,6 +154,11 @@
 
     def seat(axis, place):
         return device(*(place if k == axis else a for k, a in enumerate(at)))
+
+    def opens(m):
+        if m and ROUND[m] == ROUND[m - 1]:
+            return 0
+        return sum(count for (_, _, count), r in zip(PARTS, ROUND) if r == ROUND[m])
 
     def piece(m):
         n, skip, count = PARTS[m]
@@ -162,7 +172,7 @@
         dst = pl.ds(STARTS[n] // 2, 2 * count)
         remote(
             (own_d.at[src], one_d.at[dst]), (own_c.at[src], one_c.at[dst]),
-            send1, recv1.at[n], seat(axis, others(axis)[near]),
+            send1, recv1.at[ROUND[n]], seat(axis, others(axis)[near]),
         )
 
     def keep_send(n, rel):
@@ -172,7 +182,7 @@
         dst = pl.ds((STARTS[n] - STARTS[KEPT]) // 4 * 3 + (rel - 1) * count, count)
         remote(
             (own_d.at[src], keep_d.at[dst]), (own_c.at[src], keep_c.at[dst]),
-            send1, recv1.at[n], seat(axis, others(axis)[rel]),
+            send1, recv1.at[ROUND[n]], seat(axis, others(axis)[rel]),
         )
 
     def meet_part(m, start):
@@ -198,8 +208,11 @@
 
     for n, (stream, off) in enumerate(CHUNKS):
         start, size = chunk(stream, off)
-        with jax.named_scope(f"core_wait#n={n}"):
-            wait_bytes(got_d, size * 5 // 2, core_recv.at[n])
+        together = 1 if n < 6 else 3
+        if n % together == 0:
+            several = sum(4 * COUNT[s] for s, _ in CHUNKS[n : n + together])
+            with jax.named_scope(f"core_wait#n={n}"):
+                wait_bytes(got_d, several * 5 // 2, core_recv.at[slot_of(n)])
         for m in range(len(PARTS)):
             if PARTS[m][0] == n:
                 meet_part(m, start)
@@ -217,8 +230,9 @@
         mine, theirs = places[0], places[near]
         rest = at[second] * STRIDE[second] + at[third] * STRIDE[third]
         lower = jnp.where(theirs < mine, 1, 0)
-        with jax.named_scope(f"wait1#n={n}"):
-            wait_bytes(one_d, 5 * count, recv1.at[n])
+        if opens(n):
+            with jax.named_scope(f"wait1#n={n}"):
+                wait_bytes(one_d, 5 * opens(n), recv1.at[ROUND[n]])
         for part, rel in enumerate((0, 3) if off in PLAIN else (1, 0)):
             to_d, to_c = (pass_d, pass_c) if rel else (mid_d, mid_c)
             base = STARTS[n] // 4
@@ -239,15 +253,16 @@
         part = pl.ds(STARTS[n] // 4, count)
         remote(
             (pass_d.at[part], met_d.at[part]), (pass_c.at[part], met_c.at[part]),
-            send1b, recv1b.at[n], seat(first, places[away]),
+            send1b, recv1b.at[ROUND[n]], seat(first, places[away]),
         )
 
     def second_join(n):
         stream, off, skip, count = piece(n)
         second = ORDER[stream][1]
         base, into = STARTS[n] // 4, BASE[stream] // 4 + (off - 1) * COUNT[stream] + skip
-        with jax.named_scope(f"wait1b#n={n}"):
-            wait_bytes(one_d, 3 * count, recv1b.at[n])
+        if opens(n):
+            with jax.named_scope(f"wait1b#n={n}"):
+                wait_bytes(one_d, 3 * opens(n), recv1b.at[ROUND[n]])
 
         def join(t, carry):
             q = base + t
@@ -266,8 +281,9 @@
         into = BASE[stream] // 4 + at[second] * count
         places = others(first)
         rest = at[second] * STRIDE[second] + at[third] * STRIDE[third]
-        with jax.named_scope(f"keep_wait#n={n}"):
-            wait_bytes(own_c, 5 * count, recv1.at[n])
+        if opens(n):
+            with jax.named_scope(f"keep_wait#n={n}"):
+                wait_bytes(own_c, 5 * opens(n), recv1.at[ROUND[n]])
 
         def join(t, carry):
             best = tag = color = None
@@ -392,7 +408,7 @@
     for tiles, channels in ((128, 3), (128, 3), (128, 3), (48, 3), (24, 4), (24, 4), (24, 4), (24, 3), (32, 4), (32, 4), (8, 4), (6, 4)):
         scratch += [pltpu.VMEM((tiles, 16, 128), i32), pltpu.VMEM((tiles, channels, 16, 128), bf16)]
     scratch += [pltpu.VMEM((128, 2, 128), jnp.float32), dma((2,)), dma]
-    scratch += [dma((2,)), dma((12,)), dma((2,)), dma((len(PARTS),)), dma((2,)), dma((KEPT,)), dma((2,)), dma((3,)), dma((2,)), dma]
+    scratch += [dma((2,)), dma((8,)), dma((2,)), dma((len(ROUNDS),)), dma((2,)), dma((len(ROUNDS) - 1,)), dma((2,)), dma((3,)), dma((2,)), dma]
     scratch += [dma, dma]
     depth, color, thumbs = pl.pallas_call(
         kernel,

time: 37.8 us -> 37.5 us (level)
  no operation moved by 1% of the time
where the time goes in v8:
time: 37.5 us; the launch traced here: 37.3 us
  Pallas kernels  36.7 us (98%)
  between operations  0.65 us (2%)
    pallas_call x1, Pallas kernels, shards(): pl.pallas_call(kernel, out_shape=(pltpu.VMEM((2, 16, 128), i32), pltpu.VM...  35.7 us
    pallas_call x1, Pallas kernels, shards(): pl.pallas_call(settle, out_shape=(jax.ShapeDtypeStruct((2, 16, 128), i32)...  0.99 us

profile of v8, /device:TPU:1, one launch (start us, length us, event | category | flops | bytes accessed | tf_op | source)
XLA Modules:
  0.0 37.3 jit_solution(1810386647997417548)
XLA Ops:
  0.6 0.0 copy-start
  0.6 35.7 %composite.1 = (s32[2,16,128]{2,1,0:T(8,128)S(1)}, bf16[2,3,16,128]{3,2,1,0:T(8,128)(2,1)S(1)}, f32[128,2,128]{2,1,0:T(2,128)S(1)}) custom-call(s32[1,128]{1,0:T(1,128)} %tiles_ref.1, s32[1,128]{1,0:T(1,128)} %bitcast.12, s32[1,128]{1,0:T(1,128)} %constant.2.clone.place_ref, s32[128,16,128]{2,1,0:T(8,128)} %bitcast.15, bf16[128,3,16,128]{3,2,1,0:T(8,128)(2,1)} %bitcast.14), custom_call_target="tpu_custom_call" | custom-call | tf_op jit(solution)/shard_map/composite/pallas_call | solution.py:413
  36.3 0.0 copy-done
  36.3 1.0 %settle.1 = (s32[2,16,128]{2,1,0:T(8,128)}, bf16[2,3,16,128]{3,2,1,0:T(8,128)(2,1)}, f32[192,128]{1,0:T(8,128)}) custom-call(s32[1,128]{1,0:T(1,128)S(1)} %bitcast.13, s32[2,16,128]{2,1,0:T(8,128)S(1)} %get-tuple-element.9.depth_ref, bf16[2,3,16,128]{3,2,1,0:T(8,128)(2,1)S(1)} %get-tuple-element.10.color_ref, f32[128,2,128]{2,1,0:T(2,128)S(1)} %get-tuple-element.11.thumbs_ref), custom_call_target="tpu_custom_call" | custom-call | tf_op jit(solution)/shard_map/settle/pallas_call | solution.py:432
Async XLA Ops:
  0.6 35.7 %copy-start = (s32[128]{0:T(128)S(1)}, s32[128]{0:T(128)}, u32[]{:S(2)}) copy-start(s32[128]{0:T(128)} %param.6) | copy-start | bytes 1540

commit v9 on v8

--- a/solution.py
+++ b/solution.py
@@ -35,6 +35,7 @@
 KEPT = len(PARTS) - 3
 ROUNDS = sorted({(n // 3, t if n < 9 else 0) for n, t, _ in PARTS})
 ROUND = tuple(ROUNDS.index((n // 3, t)) for n, t, _ in PARTS)
+TURNS = tuple((n, turn) for turn in range(2) for n in range(12))
 FAR_FIRST = sorted(np.ndindex(4, 4, 4), key=lambda d: -sum(min(a, 4 - a) for a in d))
 
 
@@ -131,26 +132,41 @@
         size = 4 * COUNT[stream]
         return BASE[stream] + lax.rem(at[ORDER[stream][1]] + off, 4) * size, size
 
-    def slot_of(n):
-        return n if n < 6 else 4 + n // 3
-
-    for n, (stream, off) in enumerate(CHUNKS):
-        start, size = chunk(stream, off)
-
-        def pack(t, carry):
-            q = start + t
-            slot = table[1 - core, q]
-            send_d[q] = in_d[slot]
-            send_c[q] = in_c[slot]
-            return carry
-
-        lax.fori_loop(0, size, pack, 0, unroll=4)
-        part = pl.ds(start, size)
-        remote((send_d.at[part], got_d.at[part]), (send_c.at[part], got_c.at[part]), core_send, core_recv.at[slot_of(n)], partner)
-
     def others(axis):
         c = at[axis]
         return c, c + 1 - 2 * lax.rem(c, 2), lax.rem(c + 2, 4), 3 - c
+
+    def legs(n, turn):
+        off = CHUNKS[n][1]
+        early = (1, 2) if off in PLAIN else (2, 3) if off else (3,)
+        return early if turn == 0 else tuple(r for r in range(4) if r not in early)
+
+    def slot_of(n, turn):
+        return 8 + n // 3 if turn else n if n < 6 else 4 + n // 3
+
+    def tiles_at(n, rel):
+        stream, off = CHUNKS[n]
+        return chunk(stream, off)[0] + others(ORDER[stream][0])[rel] * COUNT[stream]
+
+    def give(n, turn):
+        for rel in legs(n, turn):
+            start, count = tiles_at(n, rel), COUNT[CHUNKS[n][0]]
+
+            def pack(t, carry):
+                slot = table[1 - core, start + t]
+                send_d[start + t] = in_d[slot]
+                send_c[start + t] = in_c[slot]
+                return carry
+
+            lax.fori_loop(0, count, pack, 0, unroll=True)
+            part = pl.ds(start, count)
+            remote(
+                (send_d.at[part], got_d.at[part]), (send_c.at[part], got_c.at[part]),
+                core_send, core_recv.at[slot_of(n, turn)], partner,
+            )
+
+    for n in range(12):
+        give(n, 0)
 
     def seat(axis, place):
         return device(*(place if k == axis else a for k, a in enumerate(at)))
@@ -185,37 +201,38 @@
             send1, recv1.at[ROUND[n]], seat(axis, others(axis)[rel]),
         )
 
-    def meet_part(m, start):
-        stream, off, skip, count = piece(m)
-        places = others(ORDER[stream][0])
-        for rel in (3, 2, 1, 0) if off not in PLAIN else (1, 2, 3, 0):
-            first, into = start + places[rel] * COUNT[stream] + skip, STARTS[m] + rel * count
-
-            def meet(t, carry):
-                slot = table[core, first + t]
-                mine = (in_d[slot] - FAR) * 2 + core
-                other = (got_d[first + t] - FAR) * 2 + (1 - core)
-                nearer = other < mine
-                own_d[into + t] = jnp.where(nearer, other, mine)
-                own_c[into + t] = pick(nearer, got_c[first + t], in_c[slot])
-                return carry
-
-            lax.fori_loop(0, count, meet, 0, unroll=True)
-            if rel == 2 and off:
-                first_send(m)
-            if rel == 3 and not off:
-                keep_send(m, rel)
-
-    for n, (stream, off) in enumerate(CHUNKS):
-        start, size = chunk(stream, off)
-        together = 1 if n < 6 else 3
+    def meet_part(m, rel):
+        n, skip, count = PARTS[m]
+        first, into = tiles_at(n, rel) + skip, STARTS[m] + rel * count
+
+        def meet(t, carry):
+            slot = table[core, first + t]
+            mine = (in_d[slot] - FAR) * 2 + core
+            other = (got_d[first + t] - FAR) * 2 + (1 - core)
+            nearer = other < mine
+            own_d[into + t] = jnp.where(nearer, other, mine)
+            own_c[into + t] = pick(nearer, got_c[first + t], in_c[slot])
+            return carry
+
+        lax.fori_loop(0, count, meet, 0, unroll=True)
+
+    for n, turn in TURNS:
+        if turn == 0 and n in (3, 6, 7, 8):
+            for k in {3: range(3), 6: range(3, 6), 7: range(6, 9), 8: range(9, 12)}[n]:
+                give(k, 1)
+        together = 1 if n < 6 and turn == 0 else 3
         if n % together == 0:
-            several = sum(4 * COUNT[s] for s, _ in CHUNKS[n : n + together])
-            with jax.named_scope(f"core_wait#n={n}"):
-                wait_bytes(got_d, several * 5 // 2, core_recv.at[slot_of(n)])
+            several = sum(COUNT[CHUNKS[k][0]] * len(legs(k, turn)) for k in range(n, n + together))
+            with jax.named_scope(f"core_wait#n={n}#t={turn}"):
+                wait_bytes(got_d, several * 5 // 2, core_recv.at[slot_of(n, turn)])
         for m in range(len(PARTS)):
             if PARTS[m][0] == n:
-                meet_part(m, start)
+                for rel in legs(n, turn):
+                    meet_part(m, rel)
+                if turn == 0 and m < KEPT:
+                    first_send(m)
+                elif turn == 0:
+                    keep_send(m, 3)
 
     def closer(depth, color, best, kept):
         tag, old = color[3].astype(jnp.float32), kept[3].astype(jnp.float32)
@@ -408,7 +425,7 @@
     for tiles, channels in ((128, 3), (128, 3), (128, 3), (48, 3), (24, 4), (24, 4), (24, 4), (24, 3), (32, 4), (32, 4), (8, 4), (6, 4)):
         scratch += [pltpu.VMEM((tiles, 16, 128), i32), pltpu.VMEM((tiles, channels, 16, 128), bf16)]
     scratch += [pltpu.VMEM((128, 2, 128), jnp.float32), dma((2,)), dma]
-    scratch += [dma((2,)), dma((8,)), dma((2,)), dma((len(ROUNDS),)), dma((2,)), dma((len(ROUNDS) - 1,)), dma((2,)), dma((3,)), dma((2,)), dma]
+    scratch += [dma((2,)), dma((12,)), dma((2,)), dma((len(ROUNDS),)), dma((2,)), dma((len(ROUNDS) - 1,)), dma((2,)), dma((3,)), dma((2,)), dma]
     scratch += [dma, dma]
     depth, color, thumbs = pl.pallas_call(
         kernel,

time: 37.5 us -> 36.9 us (0.984)
  Pallas kernels: 36.7 us -> 36.1 us
    pallas_call x1, Pallas kernels: 35.7 us -> 35.1 us  [shards(): pl.pallas_call(kernel, out_shape=(pltpu.VMEM((2, 16, 128), i32), pltpu.VM...]
where the time goes in v9:
time: 36.9 us; the launch traced here: 36.8 us
  Pallas kernels  36.1 us (98%)
  between operations  0.65 us (2%)
    pallas_call x1, Pallas kernels, shards(): pl.pallas_call(kernel, out_shape=(pltpu.VMEM((2, 16, 128), i32), pltpu.VM...  35.1 us
    pallas_call x1, Pallas kernels, shards(): pl.pallas_call(settle, out_shape=(jax.ShapeDtypeStruct((2, 16, 128), i32)...  0.99 us

profile of v9, /device:TPU:1, one launch (start us, length us, event | category | flops | bytes accessed | tf_op | source)
XLA Modules:
  0.0 36.8 jit_solution(14002906443574395049)
XLA Ops:
  0.6 0.0 copy-start
  0.6 35.1 %composite.1 = (s32[2,16,128]{2,1,0:T(8,128)S(1)}, bf16[2,3,16,128]{3,2,1,0:T(8,128)(2,1)S(1)}, f32[128,2,128]{2,1,0:T(2,128)S(1)}) custom-call(s32[1,128]{1,0:T(1,128)} %tiles_ref.1, s32[1,128]{1,0:T(1,128)} %bitcast.12, s32[1,128]{1,0:T(1,128)} %constant.2.clone.place_ref, s32[128,16,128]{2,1,0:T(8,128)} %bitcast.15, bf16[128,3,16,128]{3,2,1,0:T(8,128)(2,1)} %bitcast.14), custom_call_target="tpu_custom_call" | custom-call | tf_op jit(solution)/shard_map/composite/pallas_call | solution.py:430
  35.8 0.0 copy-done
  35.8 1.0 %settle.1 = (s32[2,16,128]{2,1,0:T(8,128)}, bf16[2,3,16,128]{3,2,1,0:T(8,128)(2,1)}, f32[192,128]{1,0:T(8,128)}) custom-call(s32[1,128]{1,0:T(1,128)S(1)} %bitcast.13, s32[2,16,128]{2,1,0:T(8,128)S(1)} %get-tuple-element.9.depth_ref, bf16[2,3,16,128]{3,2,1,0:T(8,128)(2,1)S(1)} %get-tuple-element.10.color_ref, f32[128,2,128]{2,1,0:T(2,128)S(1)} %get-tuple-element.11.thumbs_ref), custom_call_target="tpu_custom_call" | custom-call | tf_op jit(solution)/shard_map/settle/pallas_call | solution.py:449
Async XLA Ops:
  0.6 35.1 %copy-start = (s32[128]{0:T(128)S(1)}, s32[128]{0:T(128)}, u32[]{:S(2)}) copy-start(s32[128]{0:T(128)} %param.6) | copy-start | bytes 1540

commit v10 on v9

--- a/solution.py
+++ b/solution.py
@@ -60,9 +60,9 @@
 
 
 def kernel(
-    tiles_ref, owner_ref, place_ref, depth_hbm, color_hbm,
+    tiles_hbm, owner_hbm, place_hbm, depth_hbm, color_hbm,
     depth_out, color_out, thumbs_out,
-    in_d, in_c, table_v, table, send_d, send_c, got_d, got_c,
+    tiles_ref, owner_ref, place_ref, in_d, in_c, table_v, table, send_d, send_c, got_d, got_c,
     own_d, own_c, one_d, one_c, mid_d, mid_c, pass_d, pass_c, met_d, met_c, keep_d, keep_c, out1_d, out1_c, two_d, two_c, out2_d, out2_c,
     last_d, last_c, thumbs,
     load_sem, table_sem, core_send, core_recv, send1, recv1, send1b, recv1b, send2, recv2, send3, recv3,
@@ -82,11 +82,15 @@
 
     partner = device(*at, c=1 - core)
 
+    smalls = [
+        pltpu.make_async_copy(src, dst, load_sem.at[2 + n])
+        for n, (src, dst) in enumerate(((tiles_hbm, tiles_ref), (owner_hbm, owner_ref), (place_hbm, place_ref)))
+    ]
     loads = [
         pltpu.make_async_copy(depth_hbm, in_d.at[pl.ds(0, 128)], load_sem.at[0]),
         pltpu.make_async_copy(color_hbm, in_c.at[pl.ds(0, 128)], load_sem.at[1]),
     ]
-    for load in loads:
+    for load in smalls + loads:
         load.start()
     barrier = pltpu.get_barrier_semaphore()
     pl.semaphore_signal(barrier, inc=1, device_id=partner, device_id_type=MESH)
@@ -96,6 +100,9 @@
 
     in_d[128] = jnp.full((16, 128), FAR, jnp.int32)
     in_c[128] = jnp.zeros((3, 16, 128), jnp.bfloat16)
+    with jax.named_scope("small_wait"):
+        for load in smalls:
+            load.wait()
     tiles = tiles_ref[...]
     live = tiles >= 0
     row = lax.shift_right_arithmetic(tiles, 4)
@@ -418,13 +425,13 @@
     vmem = pl.BlockSpec(memory_space=pltpu.VMEM)
     anywhere = pl.BlockSpec(memory_space=pl.ANY)
     dma = pltpu.SemaphoreType.DMA
-    scratch = [
+    scratch = [pltpu.VMEM((1, 128), i32)] * 3 + [
         pltpu.VMEM((129, 16, 128), i32), pltpu.VMEM((129, 3, 16, 128), bf16),
         pltpu.VMEM((2, 128), i32), pltpu.SMEM((2, 128), i32),
     ]
     for tiles, channels in ((128, 3), (128, 3), (128, 3), (48, 3), (24, 4), (24, 4), (24, 4), (24, 3), (32, 4), (32, 4), (8, 4), (6, 4)):
         scratch += [pltpu.VMEM((tiles, 16, 128), i32), pltpu.VMEM((tiles, channels, 16, 128), bf16)]
-    scratch += [pltpu.VMEM((128, 2, 128), jnp.float32), dma((2,)), dma]
+    scratch += [pltpu.VMEM((128, 2, 128), jnp.float32), dma((5,)), dma]
     scratch += [dma((2,)), dma((12,)), dma((2,)), dma((len(ROUNDS),)), dma((2,)), dma((len(ROUNDS) - 1,)), dma((2,)), dma((3,)), dma((2,)), dma]
     scratch += [dma, dma]
     depth, color, thumbs = pl.pallas_call(
@@ -434,7 +441,7 @@
             pltpu.VMEM((2, 3, 16, 128), bf16),
             pltpu.VMEM((128, 2, 128), jnp.float32),
         ),
-        in_specs=[vmem, vmem, vmem, anywhere, anywhere],
+        in_specs=[anywhere] * 5,
         out_specs=(vmem, vmem, vmem),
         scratch_shapes=scratch,
         compiler_params=pltpu.CompilerParams(collective_id=0, has_side_effects=True),

time: 36.9 us -> 36.3 us (0.984)
  Pallas kernels: 36.1 us -> 35.5 us
    pallas_call x1, Pallas kernels: 35.1 us -> 34.5 us  [shards(): pl.pallas_call(kernel, out_shape=(pltpu.VMEM((2, 16, 128), i32), pltpu.VM...]
where the time goes in v10:
time: 36.3 us; the launch traced here: 36.1 us
  Pallas kernels  35.5 us (98%)
  between operations  0.65 us (2%)
    pallas_call x1, Pallas kernels, shards(): pl.pallas_call(kernel, out_shape=(pltpu.VMEM((2, 16, 128), i32), pltpu.VM...  34.5 us
    pallas_call x1, Pallas kernels, shards(): pl.pallas_call(settle, out_shape=(jax.ShapeDtypeStruct((2, 16, 128), i32)...  0.99 us

profile of v10, /device:TPU:1, one launch (start us, length us, event | category | flops | bytes accessed | tf_op | source)
XLA Modules:
  0.0 36.1 jit_solution(7699961393251102362)
XLA Ops:
  0.6 0.0 copy-start
  0.6 34.5 %composite.1 = (s32[2,16,128]{2,1,0:T(8,128)S(1)}, bf16[2,3,16,128]{3,2,1,0:T(8,128)(2,1)S(1)}, f32[128,2,128]{2,1,0:T(2,128)S(1)}) custom-call(s32[1,128]{1,0:T(1,128)} %tiles_hbm.1, s32[1,128]{1,0:T(1,128)} %bitcast.12, s32[1,128]{1,0:T(1,128)} %constant.2.clone.place_hbm, s32[128,16,128]{2,1,0:T(8,128)} %bitcast.15, bf16[128,3,16,128]{3,2,1,0:T(8,128)(2,1)} %bitcast.14), custom_call_target="tpu_custom_call" | custom-call | tf_op jit(solution)/shard_map/composite/pallas_call | solution.py:437
  35.1 0.0 copy-done
  35.2 1.0 %settle.1 = (s32[2,16,128]{2,1,0:T(8,128)}, bf16[2,3,16,128]{3,2,1,0:T(8,128)(2,1)}, f32[192,128]{1,0:T(8,128)}) custom-call(s32[1,128]{1,0:T(1,128)S(1)} %bitcast.13, s32[2,16,128]{2,1,0:T(8,128)S(1)} %get-tuple-element.9.depth_ref, bf16[2,3,16,128]{3,2,1,0:T(8,128)(2,1)S(1)} %get-tuple-element.10.color_ref, f32[128,2,128]{2,1,0:T(2,128)S(1)} %get-tuple-element.11.thumbs_ref), custom_call_target="tpu_custom_call" | custom-call | tf_op jit(solution)/shard_map/settle/pallas_call | solution.py:456
Async XLA Ops:
  0.6 34.5 %copy-start = (s32[128]{0:T(128)S(1)}, s32[128]{0:T(128)}, u32[]{:S(2)}) copy-start(s32[128]{0:T(128)} %param.6) | copy-start | bytes 1540

commit v11 on v10

--- a/solution.py
+++ b/solution.py
@@ -83,13 +83,14 @@
     partner = device(*at, c=1 - core)
 
     smalls = [
-        pltpu.make_async_copy(src, dst, load_sem.at[2 + n])
+        pltpu.make_async_copy(src, dst, load_sem.at[n])
         for n, (src, dst) in enumerate(((tiles_hbm, tiles_ref), (owner_hbm, owner_ref), (place_hbm, place_ref)))
     ]
-    loads = [
-        pltpu.make_async_copy(depth_hbm, in_d.at[pl.ds(0, 128)], load_sem.at[0]),
-        pltpu.make_async_copy(color_hbm, in_c.at[pl.ds(0, 128)], load_sem.at[1]),
-    ]
+    loads = []
+    for n in range(4):
+        part = pl.ds(32 * n, 32)
+        loads.append(pltpu.make_async_copy(depth_hbm.at[part], in_d.at[part], load_sem.at[3 + 2 * n]))
+        loads.append(pltpu.make_async_copy(color_hbm.at[part], in_c.at[part], load_sem.at[4 + 2 * n]))
     for load in smalls + loads:
         load.start()
     barrier = pltpu.get_barrier_semaphore()
@@ -431,7 +432,7 @@
     ]
     for tiles, channels in ((128, 3), (128, 3), (128, 3), (48, 3), (24, 4), (24, 4), (24, 4), (24, 3), (32, 4), (32, 4), (8, 4), (6, 4)):
         scratch += [pltpu.VMEM((tiles, 16, 128), i32), pltpu.VMEM((tiles, channels, 16, 128), bf16)]
-    scratch += [pltpu.VMEM((128, 2, 128), jnp.float32), dma((5,)), dma]
+    scratch += [pltpu.VMEM((128, 2, 128), jnp.float32), dma((11,)), dma]
     scratch += [dma((2,)), dma((12,)), dma((2,)), dma((len(ROUNDS),)), dma((2,)), dma((len(ROUNDS) - 1,)), dma((2,)), dma((3,)), dma((2,)), dma]
     scratch += [dma, dma]
     depth, color, thumbs = pl.pallas_call(

time: 36.3 us -> 36.3 us (level)
  no operation moved by 1% of the time
where the time goes in v11:
time: 36.3 us; the launch traced here: 36.1 us
  Pallas kernels  35.5 us (98%)
  between operations  0.65 us (2%)
    pallas_call x1, Pallas kernels, shards(): pl.pallas_call(kernel, out_shape=(pltpu.VMEM((2, 16, 128), i32), pltpu.VM...  34.5 us
    pallas_call x1, Pallas kernels, shards(): pl.pallas_call(settle, out_shape=(jax.ShapeDtypeStruct((2, 16, 128), i32)...  0.99 us

profile of v11, /device:TPU:1, one launch (start us, length us, event | category | flops | bytes accessed | tf_op | source)
XLA Modules:
  0.0 36.1 jit_solution(13246467635752257624)
XLA Ops:
  0.6 0.0 copy-start
  0.6 34.5 %composite.1 = (s32[2,16,128]{2,1,0:T(8,128)S(1)}, bf16[2,3,16,128]{3,2,1,0:T(8,128)(2,1)S(1)}, f32[128,2,128]{2,1,0:T(2,128)S(1)}) custom-call(s32[1,128]{1,0:T(1,128)} %tiles_hbm.1, s32[1,128]{1,0:T(1,128)} %bitcast.12, s32[1,128]{1,0:T(1,128)} %constant.2.clone.place_hbm, s32[128,16,128]{2,1,0:T(8,128)} %bitcast.15, bf16[128,3,16,128]{3,2,1,0:T(8,128)(2,1)} %bitcast.14), custom_call_target="tpu_custom_call" | custom-call | tf_op jit(solution)/shard_map/composite/pallas_call | solution.py:438
  35.1 0.0 copy-done
  35.2 1.0 %settle.1 = (s32[2,16,128]{2,1,0:T(8,128)}, bf16[2,3,16,128]{3,2,1,0:T(8,128)(2,1)}, f32[192,128]{1,0:T(8,128)}) custom-call(s32[1,128]{1,0:T(1,128)S(1)} %bitcast.13, s32[2,16,128]{2,1,0:T(8,128)S(1)} %get-tuple-element.9.depth_ref, bf16[2,3,16,128]{3,2,1,0:T(8,128)(2,1)S(1)} %get-tuple-element.10.color_ref, f32[128,2,128]{2,1,0:T(2,128)S(1)} %get-tuple-element.11.thumbs_ref), custom_call_target="tpu_custom_call" | custom-call | tf_op jit(solution)/shard_map/settle/pallas_call | solution.py:457
Async XLA Ops:
  0.6 34.5 %copy-start = (s32[128]{0:T(128)S(1)}, s32[128]{0:T(128)}, u32[]{:S(2)}) copy-start(s32[128]{0:T(128)} %param.6) | copy-start | bytes 1540
